TPU v7x, 16 devices: a 4x2x1 block of a 4x4x8 slice. The times are simulated.
16 devices in a mesh: dp: 2 (over y, z), tp: 8 (over x, core).
Axes of the slice: x: 4, y: 2, z: 1, core: 2. Of those that a mesh axis runs over, the one named last changes fastest.
The devices are a block of a 4x4x8 slice.
Arguments:
- x: bfloat16 [2048, 1024], P('dp'), parts along dimension 0
- k_cache: bfloat16 [2048, 64, 16, 64], P('dp', None, 'tp'), parts along dimension 0
- v_cache: bfloat16 [2048, 64, 16, 64], P('dp', None, 'tp'), parts along dimension 0
- positions: int32 [2048], P('dp'), parts along dimension 0
- att_ids: int32 [2048, 2], P('dp'), parts along dimension 0
- mlp_ids: int32 [2048, 2], P('dp'), parts along dimension 0
- norm_att: float32 [1024], replicated
- w_kv: bfloat16 [1024, 16, 128], P(None, 'tp')
- router_att: bfloat16 [1024, 16], replicated
- w_query: bfloat16 [16, 1024, 1024], P(None, None, 'tp')
- w_out: bfloat16 [16, 1024, 1024], P(None, 'tp')
- norm_mlp: float32 [1024], replicated
- router_mlp: bfloat16 [1024, 32], replicated
- w_gate: bfloat16 [32, 1024, 2048], P('tp')
- w_up: bfloat16 [32, 1024, 2048], P('tp')
- w_down: bfloat16 [32, 2048, 1024], P('tp')
Outputs:
- output 1: bfloat16 [2048, 1024], P('dp'), parts along dimension 0
- output 2: bfloat16 [2048, 64, 16, 64], P('dp', None, 'tp'), parts along dimension 0
- output 3: bfloat16 [2048, 64, 16, 64], P('dp', None, 'tp'), parts along dimension 0
There are 2 independent parts. A program takes and returns all parts, laid end to end along the dimension named above; an argument that names none is the same for every part.
All inputs are finite; a program needn't handle non-finite values.
Results may differ from a plain program's by a relative error of at most 0.01323.
Values are sent between devices in bfloat16 or wider.
A program may use at most 768 MiB of HBM per device.

v0:
```python
import jax
import jax.numpy as jnp
from jax import lax
from jax.sharding import PartitionSpec as P

NORM_EPS = 1e-6
ROPE_BASE = 10000.0


def rms_norm(x, gain):
    values = x.astype(jnp.float32)
    inv_rms = lax.rsqrt(jnp.mean(values * values, axis=-1, keepdims=True) + NORM_EPS)
    return (values * inv_rms * gain).astype(jnp.bfloat16)


def rope_tables(positions, head_dim):
    half_dim = head_dim // 2
    inv_freq = ROPE_BASE ** (-(jnp.arange(half_dim, dtype=jnp.float32) * 2.0 / head_dim))
    angles = positions.astype(jnp.float32)[:, None] * inv_freq[None, :]
    return jnp.cos(angles), jnp.sin(angles)


def apply_rope(vectors, cos_table, sin_table):
    half_dim = vectors.shape[-1] // 2
    first_half = vectors[..., :half_dim]
    second_half = vectors[..., half_dim:]
    return jnp.concatenate([first_half * cos_table - second_half * sin_table, second_half * cos_table + first_half * sin_table], axis=-1)


def route_weights(logits, choice_ids, first_id, count):
    pair_gates = jax.nn.softmax(jnp.take_along_axis(logits, choice_ids, axis=1), axis=-1)
    expert_index = first_id + jnp.arange(count)
    onehot = (choice_ids[:, :, None] == expert_index[None, None, :]).astype(jnp.float32)
    dense_gates = jnp.sum(onehot * pair_gates[:, :, None], axis=1)
    return onehot, dense_gates


def attention_part(hidden, k_cache, v_cache, positions, att_ids, w_kv, router_att, w_query, w_out):
    tokens = hidden.shape[0]
    head_count = k_cache.shape[2]
    head_dim = k_cache.shape[3]
    kv_new = jnp.einsum('bd,dnc->bnc', hidden, w_kv, preferred_element_type=jnp.float32)
    cos_table, sin_table = rope_tables(positions, head_dim)
    key_new = apply_rope(kv_new[:, :, :head_dim], cos_table[:, None, :], sin_table[:, None, :]).astype(jnp.bfloat16)
    value_new = kv_new[:, :, head_dim:].astype(jnp.bfloat16)
    slot_index = jnp.arange(k_cache.shape[1])
    at_slot = (slot_index[None, :] == positions[:, None])[:, :, None, None]
    keys_all = jnp.where(at_slot, key_new[:, None, :, :], k_cache)
    values_all = jnp.where(at_slot, value_new[:, None, :, :], v_cache)
    att_logits = jnp.dot(hidden, router_att, preferred_element_type=jnp.float32)
    att_onehot, att_dense = route_weights(att_logits, att_ids, 0, w_query.shape[0])
    query_all = jnp.einsum('bd,edc->bec', hidden, w_query, preferred_element_type=jnp.float32)
    query_sel = jnp.take_along_axis(query_all, att_ids[:, :, None], axis=1).reshape(tokens, 2, head_count, head_dim)
    query_rot = apply_rope(query_sel, cos_table[:, None, None, :], sin_table[:, None, None, :]).astype(jnp.bfloat16)
    scores = jnp.einsum('bknd,bsnd->bkns', query_rot, keys_all, preferred_element_type=jnp.float32) * head_dim ** -0.5
    visible = (slot_index[None, :] <= positions[:, None])[:, None, None, :]
    weights = jax.nn.softmax(jnp.where(visible, scores, -1e30), axis=-1).astype(jnp.bfloat16)
    attended = jnp.einsum('bkns,bsnd->bknd', weights, values_all, preferred_element_type=jnp.float32).astype(jnp.bfloat16).reshape(tokens, 2, head_count * head_dim)
    out_slots = jnp.einsum('bke,bkc->bec', att_onehot.astype(jnp.bfloat16), attended, preferred_element_type=jnp.float32).astype(jnp.bfloat16)
    projected = jnp.einsum('bec,ecd->bed', out_slots, w_out, preferred_element_type=jnp.float32)
    att_part = jnp.sum(att_dense[:, :, None] * projected, axis=1)
    return att_part, keys_all, values_all


def expert_part(normed, mlp_dense, w_gate, w_up, w_down):
    gate_val = jnp.einsum('bd,edf->bef', normed, w_gate, preferred_element_type=jnp.float32)
    up_val = jnp.einsum('bd,edf->bef', normed, w_up, preferred_element_type=jnp.float32)
    activation = (jax.nn.silu(gate_val) * up_val).astype(jnp.bfloat16)
    down_out = jnp.einsum('bef,efd->bed', activation, w_down, preferred_element_type=jnp.float32)
    return jnp.sum(mlp_dense[:, :, None] * down_out, axis=1)


def solution(mesh):
    def local_step(x, k_cache, v_cache, positions, att_ids, mlp_ids, norm_att, w_kv, router_att, w_query, w_out, norm_mlp, router_mlp, w_gate, w_up, w_down):
        hidden = rms_norm(x, norm_att)
        att_part, keys_all, values_all = attention_part(hidden, k_cache, v_cache, positions, att_ids, w_kv, router_att, w_query, w_out)
        att_sum = lax.psum(att_part.astype(jnp.bfloat16), 'tp').astype(jnp.float32)
        x_mid = (x.astype(jnp.float32) + att_sum).astype(jnp.bfloat16)
        normed = rms_norm(x_mid, norm_mlp)
        mlp_logits = jnp.dot(normed, router_mlp, preferred_element_type=jnp.float32)
        local_count = w_gate.shape[0]
        _, mlp_dense = route_weights(mlp_logits, mlp_ids, lax.axis_index('tp') * local_count, local_count)
        mlp_part = expert_part(normed, mlp_dense, w_gate, w_up, w_down)
        mlp_sum = lax.psum(mlp_part.astype(jnp.bfloat16), 'tp').astype(jnp.float32)
        x_out = (x_mid.astype(jnp.float32) + mlp_sum).astype(jnp.bfloat16)
        return x_out, keys_all, values_all

    token_spec = P('dp', None)
    cache_spec = P('dp', None, 'tp', None)
    expert_spec = P('tp', None, None)
    in_specs = (token_spec, cache_spec, cache_spec, P('dp'), token_spec, token_spec, P(), P(None, 'tp', None), P(), P(None, None, 'tp'), P(None, 'tp', None), P(), P(), expert_spec, expert_spec, expert_spec)
    out_specs = (token_spec, cache_spec, cache_spec)
    return jax.shard_map(local_step, mesh=mesh, in_specs=in_specs, out_specs=out_specs, check_vma=False)
```

profile of v0, /device:TPU:112, one launch (start us, length us, event | category | flops | bytes accessed | tf_op | source)
XLA Modules:
  0.0 507.3 jit_solution(7154129996484461025)
XLA Ops:
  8.0 1.5 iota_compare_fusion
  9.5 2.1 fusion.3
  11.6 1.3 copy.79
  12.9 2.4 fusion.33
  15.9 1.0 copy.83
  17.0 1.0 copy.84
  18.9 22.7 %broadcast_select_fusion = (bf16[1024,64,2,64]{0,3,2,1:T(8,128)(2,1)}, bf16[1024,64,2,64]{0,3,2,1:T(8,128)(2,1)}) fusion(bf16[1024,64,2,64]{0,3,2,1:T(8,128)(2,1)} %param.17, pred[1024,64]{0,1:T(8,128)(4,1)S(1)} %copy.78, bf16[1024,2,64]{0,2,1:T(8,128)(2,1)S(1)} %pad_maximum_fusion, bf16[1024,64,2,64]{0,3,2,1:T(8,128)(2,1)} %param.18, ...), kind=kLoop, calls=%fused_computation.9 | loop fusion | flops 16777216 | bytes 67698688 | tf_op jit(solution)/shard_map/jit(_where)/select_n | solution.py:48
  41.7 46.9 %copy.85 = bf16[1024,64,2,64]{3,1,2,0:T(8,128)(2,1)} copy(bf16[1024,64,2,64]{0,3,2,1:T(8,128)(2,1)} %get-tuple-element.11) | data formatting | bytes 33554432 | tf_op jit(solution)/shard_map/jit(_where)/select_n | solution.py:48
  88.6 0.7 fusion.35
  89.9 16.8 %gather_fusion = f32[2048]{0:T(1024)S(1)} fusion(f32[1024,16]{0,1:T(8,128)S(1)} %fusion.35, s32[2048]{0:T(1024)S(1)} %reshape.254), kind=kCustom, calls=%fused_computation | custom fusion | bytes 32768 | tf_op jit(solution)/shard_map/jit(take_along_axis)/gather | solution.py:31
  107.7 6.6 %fusion.17 = f32[1024,16,128]{2,0,1:T(8,128)S(1)} fusion(bf16[16,1024,128]{2,1,0:T(8,128)(2,1)} %param.25, bf16[1024,1024]{1,0:T(8,128)(2,1)S(1)} %copy-done.3, f32[1024]{0:T(1024)S(1)} %copy-done.23, f32[1024]{0:T(1024)S(1)} %copy-done.18), kind=kOutput, calls=%fused_computation.34 | convolution fusion | flops 4299161600 | bytes 14688256 | tf_op jit(solution)/shard_map/bd,edc->bec/dot_general | solution.py:52
  114.3 8.1 %copy.81 = f32[1024,16,128]{2,1,0:T(8,128)} copy(f32[1024,16,128]{2,0,1:T(8,128)S(1)} %fusion.17) | data formatting | bytes 16777216 | tf_op jit(solution)/shard_map/bd,edc->bec/dot_general | solution.py:52
  122.3 20.6 %gather_fusion.1 = f32[2048,128]{1,0:T(8,128)S(1)} fusion(f32[1024,16,128]{2,1,0:T(8,128)} %copy.81, s32[2048]{0:T(1024)S(1)} %reshape.254), kind=kCustom, calls=%fused_computation.1 | custom fusion | bytes 2113536 | tf_op jit(solution)/shard_map/jit(take_along_axis)/gather | solution.py:53
  142.9 2.5 gather.16
  145.4 6.7 %copy_select_fusion = f32[1024,2,2,64]{3,1,2,0:T(2,128)S(1)} fusion(f32[1024,2,2,64]{3,2,1,0:T(2,128)} %gather.16, pred[1024,2]{1,0:T(8,128)(4,1)S(1)} %copy.80), kind=kLoop, calls=%fused_computation.36 | loop fusion | flops 262144 | bytes 2099200 | tf_op jit(solution)/shard_map/jit(take_along_axis)/select_n | solution.py:53
  152.1 3.7 subtract_convert_fusion
  155.9 23.3 %multiply_select_fusion = f32[1024,2,64,2]{2,3,1,0:T(2,128)} fusion(pred[1024,64]{1,0:T(8,128)(4,1)S(1)} %copy-done.13, bf16[1024,64,2,64]{3,1,2,0:T(8,128)(2,1)} %copy.85, bf16[1024,2,2,32]{3,1,2,0:T(2,128)(2,1)} %get-tuple-element.8, bf16[1024,2,2,32]{3,1,2,0:T(2,128)(2,1)S(1)} %get-tuple-element.7), kind=kOutput, calls=%fused_computation.37 | convolution fusion | flops 35127296 | bytes 18415616 | tf_op jit(solution)/shard_map/bknd,bsnd->bkns/dot_general | solution.py:55
  179.2 7.2 %fusion.38 = (f32[1024,2,2]{1,2,0:T(2,128)S(1)}, f32[1024,2,2,64]{3,1,2,0:T(2,128)}) fusion(f32[1024,2,64,2]{2,3,1,0:T(2,128)} %multiply_select_fusion), kind=kOutput, calls=%fused_computation.82 | output fusion | flops 524351 | bytes 2113536 | tf_op jit(solution)/shard_map/sub | solution.py:57
  186.4 46.7 %copy.86 = bf16[1024,64,2,64]{3,1,2,0:T(8,128)(2,1)} copy(bf16[1024,64,2,64]{0,3,2,1:T(8,128)(2,1)} %get-tuple-element.12) | data formatting | bytes 33554432 | tf_op jit(solution)/shard_map/jit(_where)/select_n | solution.py:49
  233.2 16.0 %fusion.21 = bf16[1024,2,2,64]{3,1,2,0:T(2,128)(2,1)} fusion(bf16[1024,64,2,64]{3,1,2,0:T(8,128)(2,1)} %copy.86, f32[1024,2,2,64]{3,1,2,0:T(2,128)} %get-tuple-element.18, f32[1024,2,2]{1,2,0:T(2,128)S(1)} %get-tuple-element.17), kind=kOutput, calls=%fused_computation.42 | convolution fusion | flops 34340864 | bytes 18366464 | tf_op jit(solution)/shard_map/bkns,bsnd->bknd/dot_general | solution.py:58
  249.2 2.4 copy.87
  252.5 1.7 convolution_convert_fusion
  254.6 11.8 %fusion.1 = bf16[1024,1024]{1,0:T(8,128)(2,1)} fusion(f32[1024,16]{0,1:T(8,128)S(1)} %select_reduce_fusion, bf16[16,128,1024]{2,1,0:T(8,128)(2,1)S(1)} %copy-done.20, bf16[1024,16,128]{2,1,0:T(8,128)(2,1)S(1)} %convolution_convert_fusion), kind=kOutput, calls=%fused_computation.5 | convolution fusion | flops 4327473152 | bytes 10551296 | tf_op jit(solution)/shard_map/bec,ecd->bed/dot_general | solution.py:60
  267.6 59.2 %all-reduce.3.cloned.1.call-done = bf16[1024,1024]{1,0:T(8,128)(2,1)} async-done(((bf16[1024,1024]{1,0:T(8,128)(2,1)}), bf16[1024,1024]{1,0:T(8,128)(2,1)}) %all-reduce.3.cloned.1.call-update) | async-done | bytes 2097168 | tf_op jit(solution)/shard_map/psum | solution.py:77
  326.8 2.5 fusion.7
  329.3 2.1 fusion.9
  331.4 29.6 %fusion.13 = f32[1024,4,2048]{2,0,1:T(8,128)} fusion(bf16[4,1024,2048]{2,1,0:T(8,128)(2,1)} %param.29, bf16[1024,1024]{1,0:T(8,128)(2,1)} %fusion.9), kind=kOutput, calls=%fused_computation.28 | convolution fusion | flops 17179869184 | bytes 52428800 | tf_op jit(solution)/shard_map/bd,edf->bef/dot_general | solution.py:66
  361.7 16.8 %gather_fusion.2 = f32[2048]{0:T(1024)S(1)} fusion(f32[1024,32]{0,1:T(8,128)S(1)} %fusion.39, s32[2048]{0:T(1024)S(1)} %reshape.266), kind=kCustom, calls=%fused_computation.2 | custom fusion | bytes 32768 | tf_op jit(solution)/shard_map/jit(take_along_axis)/gather | solution.py:31
  379.3 31.3 %fusion.71 = bf16[1024,4,2048]{2,0,1:T(8,128)(2,1)} fusion(bf16[4,1024,2048]{2,1,0:T(8,128)(2,1)} %param.30, bf16[1024,1024]{1,0:T(8,128)(2,1)S(1)} %copy-done.7, f32[1024,4,2048]{2,0,1:T(8,128)} %fusion.13), kind=kOutput, calls=%bitcast_fusion.clone.1 | convolution fusion | flops 17230200832 | bytes 69206016 | tf_op jit(solution)/shard_map/bd,edf->bef/dot_general | solution.py:67
  410.7 27.3 %fusion.2 = bf16[1024,1024]{1,0:T(8,128)(2,1)} fusion(bf16[4,2048,1024]{2,1,0:T(8,128)(2,1)} %param.31, f32[1024,4]{0,1:T(4,128)S(1)} %select_reduce_fusion.1, bf16[1024,4,2048]{2,0,1:T(8,128)(2,1)} %fusion.71), kind=kOutput, calls=%fused_computation.8 | convolution fusion | flops 17187209216 | bytes 35667968 | tf_op jit(solution)/shard_map/bef,efd->bed/dot_general | solution.py:69
  438.0 57.0 %all-reduce.5.cloned.1.call-done = bf16[1024,1024]{1,0:T(8,128)(2,1)} async-done(((bf16[1024,1024]{1,0:T(8,128)(2,1)}), bf16[1024,1024]{1,0:T(8,128)(2,1)}) %all-reduce.5.cloned.1.call-update) | async-done | bytes 2097168 | tf_op jit(solution)/shard_map/psum | solution.py:84
  495.0 5.0 fusion.10
  (85 shorter events, 7.9 us)
Async XLA Ops:
  7.2 353.8 %copy-start = (bf16[1024,32]{0,1:T(8,128)(2,1)S(1)}, bf16[1024,32]{0,1:T(8,128)(2,1)}, u32[]{:S(2)}) copy-start(bf16[1024,32]{0,1:T(8,128)(2,1)} %param.28) | copy-start | bytes 196612
  7.2 319.6 %all-reduce.3.cloned.1.call-start = ((), (), s32[]{:S(2)}) async-start(), calls=%async_computation | async-start | bytes 4194304 | tf_op jit(solution)/shard_map/psum | solution.py:77
  11.6 77.0 %copy-start.17 = (f32[1024]{0:T(1024)}, f32[1024]{0:T(1024)S(1)}, u32[]{:S(2)}) copy-start(f32[1024]{0:T(1024)S(1)} %add_rsqrt_fusion.1) | copy-start | bytes 12292
  12.9 5.1 %copy-start.11 = (s32[1024,2]{0,1:T(2,128)S(1)}, s32[1024,2]{0,1:T(2,128)}, u32[]{:S(2)}) copy-start(s32[1024,2]{0,1:T(2,128)} %param.20) | copy-start | bytes 24580
  41.7 46.9 %copy-start.2 = (bf16[1024,1024]{1,0:T(8,128)(2,1)S(1)}, bf16[1024,1024]{1,0:T(8,128)(2,1)}, u32[]{:S(2)}) copy-start(bf16[1024,1024]{1,0:T(8,128)(2,1)} %param.16) | copy-start | bytes 6291460
  41.7 46.9 %copy-start.21 = (bf16[1024,16]{0,1:T(8,128)(2,1)S(1)}, bf16[1024,16]{0,1:T(8,128)(2,1)}, u32[]{:S(2)}) copy-start(bf16[1024,16]{0,1:T(8,128)(2,1)} %param.24) | copy-start | bytes 98308
  41.7 46.9 %copy-start.22 = (f32[1024]{0:T(1024)S(1)}, f32[1024]{0:T(1024)}, u32[]{:S(2)}) copy-start(f32[1024]{0:T(1024)} %param.22) | copy-start | bytes 12292
  89.8 17.5 %copy-start.12 = (s32[1024,2]{0,1:T(2,128)S(1)}, s32[1024,2]{0,1:T(2,128)}, u32[]{:S(2)}) copy-start(s32[1024,2]{0,1:T(2,128)} %param.20) | copy-start | bytes 24580
  89.8 17.8 %copy-start.3 = (bf16[1024,1024]{1,0:T(8,128)(2,1)S(1)}, bf16[1024,1024]{1,0:T(8,128)(2,1)}, u32[]{:S(2)}) copy-start(bf16[1024,1024]{1,0:T(8,128)(2,1)} %param.16) | copy-start | bytes 6291460
  89.8 17.8 %copy-start.18 = (f32[1024]{0:T(1024)S(1)}, f32[1024]{0:T(1024)}, u32[]{:S(2)}) copy-start(f32[1024]{0:T(1024)} %copy-done.17) | copy-start | bytes 12292
  89.8 17.8 %copy-start.23 = (f32[1024]{0:T(1024)S(1)}, f32[1024]{0:T(1024)}, u32[]{:S(2)}) copy-start(f32[1024]{0:T(1024)} %param.22) | copy-start | bytes 12292
  145.4 6.7 %copy-start.8 = (f32[1024,32]{1,0:T(8,128)S(1)}, f32[1024,32]{1,0:T(8,128)}, u32[]{:S(2)}) copy-start(f32[1024,32]{1,0:T(8,128)} %copy.83) | copy-start | bytes 393220
  145.4 6.7 %copy-start.9 = (f32[1024,32]{1,0:T(8,128)S(1)}, f32[1024,32]{1,0:T(8,128)}, u32[]{:S(2)}) copy-start(f32[1024,32]{1,0:T(8,128)} %copy.84) | copy-start | bytes 393220
  152.1 3.8 copy-start.13
  233.2 18.8 %copy-start.10 = (bf16[1024,2,16]{0,2,1:T(8,128)(2,1)S(1)}, bf16[1024,2,16]{0,2,1:T(8,128)(2,1)}, u32[]{:S(2)}) copy-start(bf16[1024,2,16]{0,2,1:T(8,128)(2,1)} %convert_convert_fusion) | copy-start | bytes 196612
  252.4 2.2 copy-start.20
  254.6 11.9 %copy-start.14 = (s32[1024,2]{0,1:T(2,128)S(1)}, s32[1024,2]{0,1:T(2,128)}, u32[]{:S(2)}) copy-start(s32[1024,2]{0,1:T(2,128)} %param.21) | copy-start | bytes 24580
  266.3 62.9 %copy-start.16 = (f32[1024]{0:T(1024)S(1)}, f32[1024]{0:T(1024)}, u32[]{:S(2)}) copy-start(f32[1024]{0:T(1024)} %param.27) | copy-start | bytes 12292
  266.4 228.6 %all-reduce.5.cloned.1.call-start = ((), (), s32[]{:S(2)}) async-start(), calls=%async_computation.1 | async-start | bytes 4194304 | tf_op jit(solution)/shard_map/psum | solution.py:84
  326.8 2.5 copy-start.5
  331.4 29.6 %copy-start.6 = (bf16[1024,1024]{1,0:T(8,128)(2,1)S(1)}, bf16[1024,1024]{1,0:T(8,128)(2,1)}, u32[]{:S(2)}) copy-start(bf16[1024,1024]{1,0:T(8,128)(2,1)} %fusion.9) | copy-start | bytes 6291460
  361.7 17.5 %copy-start.15 = (s32[1024,2]{0,1:T(2,128)S(1)}, s32[1024,2]{0,1:T(2,128)}, u32[]{:S(2)}) copy-start(s32[1024,2]{0,1:T(2,128)} %param.21) | copy-start | bytes 24580
  361.7 17.6 %copy-start.7 = (bf16[1024,1024]{1,0:T(8,128)(2,1)S(1)}, bf16[1024,1024]{1,0:T(8,128)(2,1)}, u32[]{:S(2)}) copy-start(bf16[1024,1024]{1,0:T(8,128)(2,1)} %fusion.9) | copy-start | bytes 6291460
  379.3 31.3 %copy-start.19 = (s32[4]{0:T(128)S(1)}, s32[4]{0:T(128)}, u32[]{:S(2)}) copy-start(s32[4]{0:T(128)} %iota_add_fusion) | copy-start | bytes 52
  410.7 84.4 %copy-start.4 = (bf16[1024,1024]{1,0:T(8,128)(2,1)S(1)}, bf16[1024,1024]{1,0:T(8,128)(2,1)}, u32[]{:S(2)}) copy-start(bf16[1024,1024]{1,0:T(8,128)(2,1)} %param.16) | copy-start | bytes 6291460
  438.0 62.0 %copy-start.1 = (bf16[1024,32]{0,1:T(8,128)(2,1)S(1)}, bf16[1024,32]{0,1:T(8,128)(2,1)}, u32[]{:S(2)}) copy-start(bf16[1024,32]{0,1:T(8,128)(2,1)} %param.28) | copy-start | bytes 196612
Sparse Core Ops, SparseCore 0:
  266.5 60.1 all-reduce.2
  438.1 56.8 all-reduce.4
where the time goes:
time: 516 us; the launch traced here: 507 us
  local copies, waits for them, and re-layouts  168 us (33%)
  matrix products  151 us (29%)
  waiting for transfers between devices  116 us (22%)
  other arithmetic  56.5 us (11%)
  between operations  15 us (3%)
    psum x1, waiting for transfers between devices, local_step(): att_sum = lax.psum(att_part.astype(jnp.bfloat16), 'tp').astype(jnp.float32)  59.2 us
    psum x1, waiting for transfers between devices, local_step(): mlp_sum = lax.psum(mlp_part.astype(jnp.bfloat16), 'tp').astype(jnp.float32)  57 us
    select_n x1, local copies, waits for them, and re-layouts, attention_part(): keys_all = jnp.where(at_slot, key_new[:, None, :, :], k_cache)  46.9 us
    select_n x1, local copies, waits for them, and re-layouts, attention_part(): values_all = jnp.where(at_slot, value_new[:, None, :, :], v_cache)  46.7 us
    gather x10, local copies, waits for them, and re-layouts, route_weights(): jnp.take_along_axis(logits, choice_ids, axis=1)  35.9 us
    dot_general x1, matrix products, expert_part(): jnp.einsum('bd,edf->bef', normed, w_up, preferred_element_type=jnp.float32)  31.3 us
    dot_general x1, matrix products, expert_part(): jnp.einsum('bd,edf->bef', normed, w_gate, preferred_element_type=jnp.floa...  29.6 us
    dot_general x1, matrix products, expert_part(): jnp.einsum('bef,efd->bed', activation, w_down, preferred_element_type=jnp...  27.3 us
  transfers between devices with their start and end apart: 2, of which 2 were waited for; matrix products, arithmetic and copies ran while one was open for 0% of the time, Pallas kernels for 0%

commit v1 on v0

v1 whole, which is shorter than its diff:
```python
import functools

import jax
import jax.numpy as jnp
from jax import lax
from jax.experimental import pallas as pl
from jax.experimental.pallas import tpu as pltpu
from jax.sharding import PartitionSpec as P

NORM_EPS = 1e-6
ROPE_BASE = 10000.0
F32 = jnp.float32
BF16 = jnp.bfloat16
MESH = pl.DeviceIdType.MESH


NEG = -1e30


def attn_kernel(x_ref, gain_ref, wkv_ref, router_ref, wq_ref, wo_ref, pos_ref, ids_ref, cos_ref, sin_ref, k_ref, v_ref, part_ref, ko_ref, vo_ref, sc_ref, sel_ref):
    block, width = x_ref.shape
    slots, heads, dim, _ = k_ref.shape
    experts = wq_ref.shape[0]
    cols = heads * dim
    half = dim // 2
    xf = x_ref[...].astype(F32)
    inv = lax.rsqrt(jnp.mean(xf * xf, axis=-1, keepdims=True) + NORM_EPS)
    hidden = (xf * inv * gain_ref[...]).astype(BF16)
    cos_t = cos_ref[...]
    sin_t = sin_ref[...]

    def rope(head):
        first, second = head[:half], head[half:]
        return jnp.concatenate([first * cos_t - second * sin_t, second * cos_t + first * sin_t], axis=0)

    kv_t = jnp.dot(hidden, wkv_ref[...], preferred_element_type=F32).T
    k_new = [rope(kv_t[n * 2 * dim:n * 2 * dim + dim]).astype(BF16) for n in range(heads)]
    v_new = [kv_t[n * 2 * dim + dim:(n + 1) * 2 * dim].astype(BF16) for n in range(heads)]

    logits = lax.dot_general(router_ref[...], hidden, (((1,), (1,)), ((), ())), preferred_element_type=F32)
    ids_row = [ids_ref[j:j + 1, :] for j in range(2)]
    expert_iota = lax.broadcasted_iota(jnp.int32, (experts, block), 0)
    picked = [jnp.sum(jnp.where(expert_iota == ids_row[j], logits, 0.0), axis=0, keepdims=True) for j in range(2)]
    top = jnp.maximum(picked[0], picked[1])
    raised = [jnp.exp(p - top) for p in picked]
    gate = [r / (raised[0] + raised[1]) for r in raised]
    ids_col = [jnp.broadcast_to(ids_row[j], (cols, block)).T for j in range(2)]
    gate_col = [jnp.broadcast_to(gate[j], (cols, block)).T for j in range(2)]

    chosen = [jnp.zeros((block, cols), F32) for _ in range(2)]
    for e in range(experts):
        q_e = jnp.dot(hidden, wq_ref[e], preferred_element_type=F32)
        chosen = [jnp.where(ids_col[j] == e, q_e, chosen[j]) for j in range(2)]
    q_rot = []
    for j in range(2):
        q_t = chosen[j].T
        q_rot.append([rope(q_t[n * dim:(n + 1) * dim]).astype(BF16).astype(F32) for n in range(heads)])

    pos = pos_ref[...]
    pos16 = jnp.broadcast_to(pos.astype(F32), (dim, block)).astype(BF16)

    def score_step(s, carry):
        at_slot = pos16 == jnp.full((dim, block), s, jnp.int32).astype(F32).astype(BF16)
        for n in range(heads):
            packed = k_ref[s, n]
            keys = packed.astype(F32)
            for j in range(2):
                sc_ref[j * heads + n, pl.ds(s, 1), :] = jnp.sum(q_rot[j][n] * keys, axis=0, keepdims=True)
            ko_ref[s, n] = jnp.where(at_slot, k_new[n], packed)
        return carry

    lax.fori_loop(0, slots, score_step, 0, unroll=4)

    slot_iota = lax.broadcasted_iota(jnp.int32, (slots, block), 0)
    here = slot_iota == pos
    visible = slot_iota <= pos
    out = []
    for j in range(2):
        for n in range(heads):
            fresh = jnp.sum(q_rot[j][n] * k_new[n].astype(F32), axis=0, keepdims=True)
            score = jnp.where(here, fresh, sc_ref[j * heads + n]) * dim ** -0.5
            score = jnp.where(visible, score, NEG)
            raised_s = jnp.exp(score - jnp.max(score, axis=0, keepdims=True))
            prob = (raised_s / jnp.sum(raised_s, axis=0, keepdims=True)).astype(BF16).astype(F32)
            own = jnp.sum(jnp.where(here, prob, 0.0), axis=0, keepdims=True)
            sc_ref[j * heads + n] = jnp.where(here, 0.0, prob)
            out.append(own * v_new[n].astype(F32))

    def value_step(s, carry):
        at_slot = pos16 == jnp.full((dim, block), s, jnp.int32).astype(F32).astype(BF16)
        carry = list(carry)
        for n in range(heads):
            packed = v_ref[s, n]
            values = packed.astype(F32)
            for j in range(2):
                i = j * heads + n
                carry[i] = carry[i] + sc_ref[i, pl.ds(s, 1), :] * values
            vo_ref[s, n] = jnp.where(at_slot, v_new[n], packed)
        return tuple(carry)

    out = lax.fori_loop(0, slots, value_step, tuple(out), unroll=4)

    total = None
    for j in range(2):
        o_j = jnp.concatenate(out[j * heads:(j + 1) * heads], axis=0).T
        for e in range(experts):
            sel_ref[:, e * cols:(e + 1) * cols] = jnp.where(ids_col[j] == e, o_j, 0.0).astype(BF16)
        projected = jnp.dot(sel_ref[...], wo_ref[...], preferred_element_type=F32)
        scaled = projected * jnp.concatenate([gate_col[j]] * (width // cols), axis=1)
        total = scaled if total is None else total + scaled
    part_ref[...] = total.astype(BF16)


def attention(x, k_cache, v_cache, positions, att_ids, norm_att, w_kv, router_att, w_query, w_out, block=128):
    tokens, width = x.shape
    _, slots, heads, dim = k_cache.shape
    experts = w_query.shape[0]
    cols = heads * dim
    half = dim // 2
    inv_freq = ROPE_BASE ** (-(jnp.arange(half, dtype=F32) * 2.0 / dim))
    angles = inv_freq[:, None] * positions.astype(F32)[None, :]
    k_t = k_cache.transpose(1, 2, 3, 0)
    v_t = v_cache.transpose(1, 2, 3, 0)
    whole = lambda *shape: pl.BlockSpec(shape, lambda i: (0,) * len(shape), pipeline_mode=pl.Buffered(1))
    lane = lambda rows: pl.BlockSpec((rows, block), lambda i: (0, i))
    cache = pl.BlockSpec((slots, heads, dim, block), lambda i: (0, 0, 0, i))
    row = pl.BlockSpec((block, width), lambda i: (i, 0))
    part, k_out, v_out = pl.pallas_call(
        attn_kernel,
        grid=(tokens // block,),
        in_specs=[row, whole(1, width), whole(width, 2 * cols), whole(experts, width), whole(experts, width, cols), whole(experts * cols, width), lane(1), lane(2), lane(half), lane(half), cache, cache],
        out_specs=[row, cache, cache],
        out_shape=[jax.ShapeDtypeStruct((tokens, width), BF16), jax.ShapeDtypeStruct(k_t.shape, BF16), jax.ShapeDtypeStruct(v_t.shape, BF16)],
        scratch_shapes=[pltpu.VMEM((2 * heads, slots, block), F32), pltpu.VMEM((block, experts * cols), BF16)],
        compiler_params=pltpu.CompilerParams(dimension_semantics=("arbitrary",), vmem_limit_bytes=56 * 1024 * 1024),
        name="attention",
    )(x, norm_att.reshape(1, width), w_kv.reshape(width, 2 * cols), router_att.T, w_query, w_out.reshape(experts * cols, width), positions.reshape(1, tokens), att_ids.T, jnp.cos(angles), jnp.sin(angles), k_t, v_t)
    return part, k_out.transpose(3, 0, 1, 2), v_out.transpose(3, 0, 1, 2)


def reduce_kernel(part_ref, resid_ref, out_ref, pair_in, ring, half_in, full_in, own, pair_sem, sems, d2d_sem):
    rows, width = part_ref.shape
    mine = rows // 2
    chips = lax.axis_size("tp") // 2
    piece = mine // chips
    halfw = width // 2
    me = lax.axis_index("tp")
    core = lax.rem(me, 2)
    chip = me // 2
    other = 1 - core
    right_chip = lax.rem(chip + 1, chips)
    left_chip = lax.rem(chip + chips - 1, chips)
    far_chip = lax.rem(chip + 2, chips)
    partner = {"tp": chip * 2 + other}
    right = {"tp": right_chip * 2 + core}
    left = {"tp": left_chip * 2 + core}

    barrier = pltpu.get_barrier_semaphore()
    for peer in (partner, right, left):
        pl.semaphore_signal(barrier, inc=1, device_id=peer, device_id_type=MESH)
    pl.semaphore_wait(barrier, 3)

    def send(src, dst, sem, peer):
        copy = pltpu.make_async_remote_copy(src_ref=src, dst_ref=dst, send_sem=sem.at[0], recv_sem=sem.at[1], device_id=peer, device_id_type=MESH)
        copy.start()
        return copy

    def block(c, q):
        return pl.ds(pl.multiple_of(c * mine + q * piece, piece), piece)

    lo, hi = pl.ds(0, halfw), pl.ds(halfw, halfw)
    order = (far_chip, right_chip, left_chip, chip)
    swaps = [send(part_ref.at[block(other, q)], pair_in.at[pl.ds(pl.multiple_of(q * piece, piece), piece)], pair_sem.at[i], partner) for i, q in enumerate(order)]

    def paired(q):
        return part_ref[block(core, q), :].astype(F32) + pair_in[pl.ds(pl.multiple_of(q * piece, piece), piece), :].astype(F32)

    swaps[0].wait_recv()
    ring[0] = paired(far_chip).astype(BF16)
    far_r = send(ring.at[0, :, lo], half_in.at[0], sems.at[0], right)
    far_l = send(ring.at[0, :, hi], half_in.at[1], sems.at[1], left)
    swaps[1].wait_recv()
    sum_r = paired(right_chip)
    ring[1, :, halfw:] = sum_r[:, halfw:].astype(BF16)
    plain_r = send(ring.at[1, :, hi], full_in.at[0, :, hi], sems.at[2], right)
    swaps[2].wait_recv()
    sum_l = paired(left_chip)
    ring[2, :, :halfw] = sum_l[:, :halfw].astype(BF16)
    plain_l = send(ring.at[2, :, lo], full_in.at[1, :, lo], sems.at[3], left)
    far_r.wait_recv()
    ring[1, :, :halfw] = (sum_r[:, :halfw] + half_in[0].astype(F32)).astype(BF16)
    added_r = send(ring.at[1, :, lo], full_in.at[0, :, lo], sems.at[4], right)
    far_l.wait_recv()
    ring[2, :, halfw:] = (sum_l[:, halfw:] + half_in[1].astype(F32)).astype(BF16)
    added_l = send(ring.at[2, :, hi], full_in.at[1, :, hi], sems.at[5], left)
    swaps[3].wait_recv()
    base = paired(chip)
    resid = resid_ref[block(core, chip), :].astype(F32)
    mine_rows = block(core, chip)
    plain_r.wait_recv()
    added_l.wait_recv()
    own[:, halfw:] = (resid[:, halfw:] + (base[:, halfw:] + full_in[0, :, halfw:].astype(F32) + full_in[1, :, halfw:].astype(F32))).astype(BF16)
    out_l = send(own.at[:, hi], out_ref.at[mine_rows, hi], sems.at[6], left)
    out_r2 = send(own.at[:, hi], out_ref.at[mine_rows, hi], sems.at[7], right)
    plain_l.wait_recv()
    added_r.wait_recv()
    own[:, :halfw] = (resid[:, :halfw] + (base[:, :halfw] + full_in[0, :, :halfw].astype(F32) + full_in[1, :, :halfw].astype(F32))).astype(BF16)
    out_r = send(own.at[:, lo], out_ref.at[mine_rows, lo], sems.at[8], right)
    out_l2 = send(own.at[:, lo], out_ref.at[mine_rows, lo], sems.at[9], left)
    out_ref[mine_rows, :] = own[...]
    d2d = [send(own, out_ref.at[mine_rows], d2d_sem.at[0], partner)]

    left_rows, right_rows, far_rows = block(core, left_chip), block(core, right_chip), block(core, far_chip)
    out_l.wait_recv()
    fwd_l = send(out_ref.at[right_rows, hi], out_ref.at[right_rows, hi], sems.at[10], left)
    out_r.wait_recv()
    fwd_r = send(out_ref.at[left_rows, lo], out_ref.at[left_rows, lo], sems.at[11], right)
    out_r2.wait_recv()
    d2d.append(send(out_ref.at[left_rows], out_ref.at[left_rows], d2d_sem.at[1], partner))
    out_l2.wait_recv()
    d2d.append(send(out_ref.at[right_rows], out_ref.at[right_rows], d2d_sem.at[2], partner))
    fwd_l.wait_recv()
    fwd_r.wait_recv()
    d2d.append(send(out_ref.at[far_rows], out_ref.at[far_rows], d2d_sem.at[3], partner))
    for copy in swaps + [far_r, far_l, plain_r, plain_l, added_r, added_l, out_l, out_r, out_r2, out_l2, fwd_l, fwd_r]:
        copy.wait_send()
    for copy in d2d:
        copy.wait()


def reduce_add(part, resid, collective_id):
    rows, width = part.shape
    mine = rows // 2
    piece = mine // (lax.axis_size("tp") // 2)
    vmem = pl.BlockSpec(memory_space=pltpu.VMEM)
    return pl.pallas_call(
        reduce_kernel,
        in_specs=[vmem, vmem],
        out_specs=vmem,
        out_shape=jax.ShapeDtypeStruct((rows, width), BF16),
        scratch_shapes=[
            pltpu.VMEM((mine, width), BF16),
            pltpu.VMEM((3, piece, width), BF16),
            pltpu.VMEM((2, piece, width // 2), BF16),
            pltpu.VMEM((2, piece, width), BF16),
            pltpu.VMEM((piece, width), BF16),
            pltpu.SemaphoreType.DMA((4, 2)),
            pltpu.SemaphoreType.DMA((12, 2)),
            pltpu.SemaphoreType.DMA((4, 2)),
        ],
        compiler_params=pltpu.CompilerParams(collective_id=collective_id, has_side_effects=True, vmem_limit_bytes=32 * 1024 * 1024),
        name="reduce_add",
    )(part, resid)


def mlp_kernel(rows, x_ref, gain_ref, router_ref, ids_ref, wg_hbm, wu_hbm, wd_hbm, y_ref, wg, wu, wd, normed, act, acc, rank_ref, gate_ref, rank_col, sem):
    tokens, width = x_ref.shape
    local, _, ffn = wg.shape
    experts = router_ref.shape[0]
    copies = []
    for e in range(local):
        copies.append([pltpu.make_async_copy(src.at[e], dst.at[e], sem.at[e, i]) for i, (src, dst) in enumerate(((wg_hbm, wg), (wu_hbm, wu), (wd_hbm, wd)))])
        for c in copies[-1]:
            c.start()

    step = 128
    for t in range(0, tokens, step):
        xf = x_ref[t:t + step, :].astype(F32)
        inv = lax.rsqrt(jnp.mean(xf * xf, axis=-1, keepdims=True) + NORM_EPS)
        normed[t:t + step, :] = (xf * inv * gain_ref[...]).astype(BF16)
    acc[...] = jnp.zeros_like(acc)

    logits = lax.dot_general(router_ref[...], normed[...], (((1,), (1,)), ((), ())), preferred_element_type=F32)
    ids_row = [ids_ref[j:j + 1, :] for j in range(2)]
    expert_iota = lax.broadcasted_iota(jnp.int32, (experts, tokens), 0)
    picked = [jnp.sum(jnp.where(expert_iota == ids_row[j], logits, 0.0), axis=0, keepdims=True) for j in range(2)]
    top = jnp.maximum(picked[0], picked[1])
    raised = [jnp.exp(p - top) for p in picked]
    gate = [r / (raised[0] + raised[1]) for r in raised]
    first = lax.axis_index("tp") * local
    local_iota = first + lax.broadcasted_iota(jnp.int32, (8, tokens), 0)
    hit = [(ids_row[j] == local_iota) for j in range(2)]
    member = jnp.where(hit[0] | hit[1], 1.0, 0.0)
    gate_ref[...] = jnp.where(hit[0], gate[0], 0.0) + jnp.where(hit[1], gate[1], 0.0)
    tri = jnp.where(lax.broadcasted_iota(jnp.int32, (step, step), 0) <= lax.broadcasted_iota(jnp.int32, (step, step), 1), 1.0, 0.0).astype(BF16)
    running = jnp.zeros((8, 1), F32)
    for t in range(0, tokens, step):
        piece = member[:, t:t + step]
        inside = jnp.dot(piece.astype(BF16), tri, preferred_element_type=F32)
        rank = jnp.where(piece > 0, inside + running - 1.0, -1.0)
        rank_ref[:, t:t + step] = rank
        rank_col[t:t + step, :] = jnp.broadcast_to(rank[:, None, :], (8, step // 8, step)).reshape(step, step).T
        running = running + jnp.sum(piece, axis=1, keepdims=True)

    for e in range(local):
        count = jnp.sum(member[e:e + 1, :]).astype(jnp.int32)
        for c in copies[e][:2]:
            c.wait()
        tiles = (count + rows - 1) // rows
        rank_row = rank_ref[e:e + 1, :]
        gate_row = gate_ref[e:e + 1, :]

        def tile_step(i, down_ready):
            base = (i * rows).astype(F32)
            hits = rank_row == lax.broadcasted_iota(jnp.int32, (rows, tokens), 0).astype(F32) + base
            gate_col = jnp.sum(jnp.where(hits, gate_row, 0.0), axis=1, keepdims=True)
            picked_rows = jnp.dot(jnp.where(hits, 1.0, 0.0).astype(BF16), normed[...], preferred_element_type=F32).astype(BF16)
            for f in range(0, ffn, 512):
                g = jnp.dot(picked_rows, wg[e, :, f:f + 512], preferred_element_type=F32)
                u = jnp.dot(picked_rows, wu[e, :, f:f + 512], preferred_element_type=F32)
                act[:, f:f + 512] = (jax.nn.silu(g) * u).astype(BF16)

            @pl.when(i == 0)
            def _():
                copies[e][2].wait()

            for t in range(0, tokens, 256):
                col = rank_col[t:t + 256, e * (step // 8):e * (step // 8) + 1]
                place = col == lax.broadcasted_iota(jnp.int32, (256, rows), 1).astype(F32) + base
                spread = jnp.where(place, 1.0, 0.0).astype(BF16)
                if t == 0:
                    down = (jnp.dot(act[...], wd[e], preferred_element_type=F32) * gate_col).astype(BF16)
                acc[t:t + 256, :] += jnp.dot(spread, down, preferred_element_type=F32)
            return down_ready

        lax.fori_loop(0, tiles, tile_step, 0)

        @pl.when(tiles == 0)
        def _():
            copies[e][2].wait()

    y_ref[...] = acc[...].astype(BF16)


def experts_mlp(x1, mlp_ids, norm_mlp, router_mlp, w_gate, w_up, w_down, rows=128):
    tokens, width = x1.shape
    local, _, ffn = w_gate.shape
    vmem = pl.BlockSpec(memory_space=pltpu.VMEM)
    hbm = pl.BlockSpec(memory_space=pl.ANY)
    return pl.pallas_call(
        functools.partial(mlp_kernel, rows),
        in_specs=[vmem, vmem, vmem, vmem, hbm, hbm, hbm],
        out_specs=vmem,
        out_shape=jax.ShapeDtypeStruct((tokens, width), BF16),
        scratch_shapes=[
            pltpu.VMEM((local, width, ffn), BF16),
            pltpu.VMEM((local, width, ffn), BF16),
            pltpu.VMEM((local, ffn, width), BF16),
            pltpu.VMEM((tokens, width), BF16),
            pltpu.VMEM((rows, ffn), BF16),
            pltpu.VMEM((tokens, width), F32),
            pltpu.VMEM((8, tokens), F32),
            pltpu.VMEM((8, tokens), F32),
            pltpu.VMEM((tokens, 128), F32),
            pltpu.SemaphoreType.DMA((local, 3)),
        ],
        compiler_params=pltpu.CompilerParams(vmem_limit_bytes=67043328),
        name="experts",
    )(x1, norm_mlp.reshape(1, width), router_mlp.T, mlp_ids.T, w_gate, w_up, w_down)


def solution(mesh):
    def local_step(x, k_cache, v_cache, positions, att_ids, mlp_ids, norm_att, w_kv, router_att, w_query, w_out, norm_mlp, router_mlp, w_gate, w_up, w_down):
        part, keys_all, values_all = attention(x, k_cache, v_cache, positions, att_ids, norm_att, w_kv, router_att, w_query, w_out)
        x_mid = reduce_add(part, x, 0)
        mlp_part = experts_mlp(x_mid, mlp_ids, norm_mlp, router_mlp, w_gate, w_up, w_down)
        x_out = reduce_add(mlp_part, x_mid, 1)
        return x_out, keys_all, values_all

    token_spec = P('dp', None)
    cache_spec = P('dp', None, 'tp', None)
    expert_spec = P('tp', None, None)
    in_specs = (token_spec, cache_spec, cache_spec, P('dp'), token_spec, token_spec, P(), P(None, 'tp', None), P(), P(None, None, 'tp'), P(None, 'tp', None), P(), P(), expert_spec, expert_spec, expert_spec)
    out_specs = (token_spec, cache_spec, cache_spec)
    return jax.shard_map(local_step, mesh=mesh, in_specs=in_specs, out_specs=out_specs, check_vma=False)
```

time: 516 us -> 148 us (0.29)
  the two profiles are of different devices: /device:TPU:112 before, /device:TPU:113 now
where the time goes in v1:
time: 148 us; the launch traced here: 146 us
  Pallas kernels  134 us (91%)
  local copies, waits for them, and re-layouts  9.32 us (6%)
  other arithmetic  1.94 us (1%)
    pallas_call x2, Pallas kernels, reduce_add(): pl.pallas_call(reduce_kernel, in_specs=[vmem, vmem], out_specs=vmem, out_...  63.6 us
    pallas_call x1, Pallas kernels, attention(): pl.pallas_call(attn_kernel, grid=(tokens // block,), in_specs=[row, whole...  50 us
    pallas_call x1, Pallas kernels, experts_mlp(): pl.pallas_call(functools.partial(mlp_kernel, rows), in_specs=[vmem, vmem,...  20.6 us
    unnamed x12, local copies, waits for them, and re-layouts  9.32 us

profile of v1, /device:TPU:113, one launch (start us, length us, event | category | flops | bytes accessed | tf_op | source)
XLA Modules:
  0.0 146.2 jit_solution(15266453387991400561)
XLA Ops:
  0.6 0.7 convert_element_type.3
  1.3 1.2 multiply_sine_fusion
  2.6 1.9 %copy.21 = bf16[128,8,2,128]{3,1,2,0:T(8,128)(2,1)} copy(bf16[128,8,2,128]{3,2,1,0:T(2,128)(2,1)} %bitcast.20) | data formatting | bytes 1048576
  4.5 0.0 copy-start.2
  4.5 50.0 %attention.1 = (bf16[1024,1024]{1,0:T(8,128)(2,1)}, bf16[64,2,64,1024]{3,2,1,0:T(8,128)(2,1)}, bf16[64,2,64,1024]{3,2,1,0:T(8,128)(2,1)}) custom-call(bf16[1024,1024]{1,0:T(8,128)(2,1)} %resid_ref.1, f32[1,1024]{1,0:T(1,128)} %bitcast.26, bf16[1024,256]{1,0:T(8,128)(2,1)} %bitcast.19, bf16[16,1024]{1,0:T(8,128)(2,1)} %bitcast.22, ...), custom_call_target="tpu_custom_call" | custom-call | tf_op jit(solution)/shard_map/attention/pallas_call | solution.py:128
  54.5 0.0 copy-done.2
  54.5 0.0 copy-start.4
  54.5 1.6 %copy-done.4 = bf16[1024,1024]{1,0:T(8,128)(2,1)S(1)} copy-done((bf16[1024,1024]{1,0:T(8,128)(2,1)S(1)}, bf16[1024,1024]{1,0:T(8,128)(2,1)}, u32[]{:S(2)}) %copy-start.4) | copy-done | bytes 2097176
  56.1 29.8 %reduce_add.2.x_ref.resid_ref = bf16[1024,1024]{1,0:T(8,128)(2,1)S(1)} custom-call(bf16[1024,1024]{1,0:T(8,128)(2,1)S(1)} %copy-done.4, bf16[1024,1024]{1,0:T(8,128)(2,1)S(1)} %copy-done.2), custom_call_target="tpu_custom_call" | custom-call | tf_op jit(solution)/shard_map/reduce_add/pallas_call | solution.py:236
  86.0 0.0 copy-start
  86.0 1.3 copy-done
  87.3 20.6 %experts.1.part_ref = bf16[1024,1024]{1,0:T(8,128)(2,1)} custom-call(bf16[1024,1024]{1,0:T(8,128)(2,1)} %copy-done, f32[1,1024]{1,0:T(1,128)} %bitcast.27, bf16[32,1024]{1,0:T(8,128)(2,1)} %bitcast.21, s32[2,1024]{1,0:T(2,128)} %bitcast.25, bf16[4,1024,2048]{2,1,0:T(8,128)(2,1)} %wg_hbm.1, bf16[4,1024,2048]{2,1,0:T(8,128)(2,1)} %wu_hbm.1, ...), custom_call_target="tpu_custom_call" | custom-call | tf_op jit(solution)/shard_map/experts/pallas_call | solution.py:340
  107.9 0.0 copy-start.1
  107.9 1.6 %copy-done.1 = bf16[1024,1024]{1,0:T(8,128)(2,1)S(1)} copy-done((bf16[1024,1024]{1,0:T(8,128)(2,1)S(1)}, bf16[1024,1024]{1,0:T(8,128)(2,1)}, u32[]{:S(2)}) %copy-start.1) | copy-done | bytes 2097176
  109.5 0.0 copy-start.3
  109.5 1.6 %copy-done.3 = bf16[1024,1024]{1,0:T(8,128)(2,1)S(1)} copy-done((bf16[1024,1024]{1,0:T(8,128)(2,1)S(1)}, bf16[1024,1024]{1,0:T(8,128)(2,1)}, u32[]{:S(2)}) %copy-start.3) | copy-done | bytes 2097176
  111.1 33.8 %reduce_add.3 = bf16[1024,1024]{1,0:T(8,128)(2,1)S(1)} custom-call(bf16[1024,1024]{1,0:T(8,128)(2,1)S(1)} %copy-done.3, bf16[1024,1024]{1,0:T(8,128)(2,1)S(1)} %copy-done.1), custom_call_target="tpu_custom_call" | custom-call | tf_op jit(solution)/shard_map/reduce_add/pallas_call | solution.py:236
  144.9 1.3 copy.23
  (1 shorter events, 0.0 us)
Async XLA Ops:
  4.5 50.0 %copy-start.2 = (bf16[1024,1024]{1,0:T(8,128)(2,1)S(1)}, bf16[1024,1024]{1,0:T(8,128)(2,1)}, u32[]{:S(2)}) copy-start(bf16[1024,1024]{1,0:T(8,128)(2,1)} %resid_ref.1) | copy-start | bytes 6291460
  54.5 1.6 %copy-start.4 = (bf16[1024,1024]{1,0:T(8,128)(2,1)S(1)}, bf16[1024,1024]{1,0:T(8,128)(2,1)}, u32[]{:S(2)}) copy-start(bf16[1024,1024]{1,0:T(8,128)(2,1)} %get-tuple-element.6.part_ref) | copy-start | bytes 6291460
  86.0 1.3 copy-start
  107.9 1.6 %copy-start.1 = (bf16[1024,1024]{1,0:T(8,128)(2,1)S(1)}, bf16[1024,1024]{1,0:T(8,128)(2,1)}, u32[]{:S(2)}) copy-start(bf16[1024,1024]{1,0:T(8,128)(2,1)} %copy-done) | copy-start | bytes 6291460
  109.5 1.6 %copy-start.3 = (bf16[1024,1024]{1,0:T(8,128)(2,1)S(1)}, bf16[1024,1024]{1,0:T(8,128)(2,1)}, u32[]{:S(2)}) copy-start(bf16[1024,1024]{1,0:T(8,128)(2,1)} %experts.1.part_ref) | copy-start | bytes 6291460

commit v2 on v1

v2 whole, which is shorter than its diff:
```python
import functools

import jax
import jax.numpy as jnp
import numpy as np
from jax import lax
from jax.experimental import pallas as pl
from jax.experimental.pallas import tpu as pltpu
from jax.sharding import PartitionSpec as P

NORM_EPS = 1e-6
ROPE_BASE = 10000.0
F32 = jnp.float32
BF16 = jnp.bfloat16
VMEM_LIMIT = 67043328
MESH = pl.DeviceIdType.MESH


NEG = -1e30


def attn_kernel(x_ref, gain_ref, wkv_ref, router_ref, wq_ref, pos_ref, ids_ref, freq_ref, k_ref, v_ref, o_ref, gate_ref, ko_ref, vo_ref, sc_ref, fold_ref, kv_ref):
    block, width = x_ref.shape
    slots, heads, dim, _ = k_ref.shape
    experts = wq_ref.shape[0]
    cols = heads * dim
    half = dim // 2
    xf = x_ref[...].astype(F32)
    inv = lax.rsqrt(jnp.mean(xf * xf, axis=-1, keepdims=True) + NORM_EPS)
    hidden = (xf * inv * gain_ref[...]).astype(BF16)
    pos = pos_ref[...]
    angles = freq_ref[...] * pos.astype(F32)
    cos_t = jnp.cos(angles)
    sin_t = jnp.sin(angles)

    @pl.when(pl.program_id(0) == 0)
    def _():
        for n in range(heads):
            kv_ref[:, n * 2 * dim:(n + 1) * 2 * dim] = wkv_ref[:, n, :]

    def rope(head):
        first, second = head[:half], head[half:]
        return jnp.concatenate([first * cos_t - second * sin_t, second * cos_t + first * sin_t], axis=0)

    kv_t = jnp.dot(hidden, kv_ref[...], preferred_element_type=F32).T
    k_new = [rope(kv_t[n * 2 * dim:n * 2 * dim + dim]).astype(BF16) for n in range(heads)]
    v_new = [kv_t[n * 2 * dim + dim:(n + 1) * 2 * dim].astype(BF16) for n in range(heads)]

    logits = lax.dot_general(router_ref[...], hidden, (((1,), (1,)), ((), ())), preferred_element_type=F32)
    ids_row = [ids_ref[j:j + 1, :] for j in range(2)]
    expert_iota = lax.broadcasted_iota(jnp.int32, (experts, block), 0)
    picked = [jnp.sum(jnp.where(expert_iota == ids_row[j], logits, 0.0), axis=0, keepdims=True) for j in range(2)]
    top = jnp.maximum(picked[0], picked[1])
    raised = [jnp.exp(p - top) for p in picked]
    gate = [r / (raised[0] + raised[1]) for r in raised]
    ids_col = [jnp.broadcast_to(ids_row[j], (cols, block)).T for j in range(2)]
    for j in range(2):
        gate_ref[j:j + 1, :] = gate[j]

    chosen = [jnp.zeros((block, cols), F32) for _ in range(2)]
    for e in range(0, experts, 2):
        q_two = jnp.dot(hidden, jnp.concatenate([wq_ref[e], wq_ref[e + 1]], axis=1), preferred_element_type=F32)
        for i in range(2):
            q_e = q_two[:, i * cols:(i + 1) * cols]
            chosen = [jnp.where(ids_col[j] == e + i, q_e, chosen[j]) for j in range(2)]
    q_rot = []
    for j in range(2):
        q_t = chosen[j].T
        q_rot.append([rope(q_t[n * dim:(n + 1) * dim]).astype(BF16).astype(F32) for n in range(heads)])

    pos16 = jnp.broadcast_to(pos.astype(F32), (dim, block)).astype(BF16)

    def score_step(s, carry):
        at_slot = pos16 == jnp.full((dim, block), s, jnp.int32).astype(F32).astype(BF16)
        for n in range(heads):
            packed = k_ref[s, n]
            keys = packed.astype(F32)
            for j in range(2):
                fold_ref[j * heads + n, pl.ds(pl.multiple_of(s * 8, 8), 8), :] = jnp.sum((q_rot[j][n] * keys).reshape(dim // 8, 8, block), axis=0)
            ko_ref[s, n] = jnp.where(at_slot, k_new[n], packed)
        return carry

    lax.fori_loop(0, slots, score_step, 0, unroll=4)

    slot_iota = lax.broadcasted_iota(jnp.int32, (slots, block), 0)
    here = slot_iota == pos
    visible = slot_iota <= pos
    out = []
    for j in range(2):
        for n in range(heads):
            fresh = jnp.sum(q_rot[j][n] * k_new[n].astype(F32), axis=0, keepdims=True)
            score = fold_ref[j * heads + n, pl.ds(0, slots, stride=8), :]
            for r in range(1, 8):
                score = score + fold_ref[j * heads + n, pl.ds(r, slots, stride=8), :]
            score = jnp.where(here, fresh, score) * dim ** -0.5
            score = jnp.where(visible, score, NEG)
            raised_s = jnp.exp(score - jnp.max(score, axis=0, keepdims=True))
            prob = (raised_s / jnp.sum(raised_s, axis=0, keepdims=True)).astype(BF16).astype(F32)
            own = jnp.sum(jnp.where(here, prob, 0.0), axis=0, keepdims=True)
            sc_ref[j * heads + n] = jnp.where(here, 0.0, prob)
            out.append(own * v_new[n].astype(F32))

    def value_step(s, carry):
        at_slot = pos16 == jnp.full((dim, block), s, jnp.int32).astype(F32).astype(BF16)
        carry = list(carry)
        for n in range(heads):
            packed = v_ref[s, n]
            values = packed.astype(F32)
            for j in range(2):
                i = j * heads + n
                carry[i] = carry[i] + sc_ref[i, pl.ds(s, 1), :] * values
            vo_ref[s, n] = jnp.where(at_slot, v_new[n], packed)
        return tuple(carry)

    out = lax.fori_loop(0, slots, value_step, tuple(out), unroll=4)

    for j in range(2):
        o_ref[j] = jnp.concatenate(out[j * heads:(j + 1) * heads], axis=0).T.astype(BF16)


def attention(x, k_cache, v_cache, positions, att_ids, norm_att, w_kv, router_att, w_query, block=128):
    tokens, width = x.shape
    _, slots, heads, dim = k_cache.shape
    experts = w_query.shape[0]
    cols = heads * dim
    half = dim // 2
    inv_freq = jnp.asarray(ROPE_BASE ** (-(np.arange(half) * 2.0 / dim)), F32)
    k_t = k_cache.transpose(1, 2, 3, 0)
    v_t = v_cache.transpose(1, 2, 3, 0)
    whole = lambda *shape: pl.BlockSpec(shape, lambda i: (0,) * len(shape), pipeline_mode=pl.Buffered(1))
    lane = lambda rows: pl.BlockSpec((rows, block), lambda i: (0, i))
    cache = pl.BlockSpec((slots, heads, dim, block), lambda i: (0, 0, 0, i))
    row = pl.BlockSpec((block, width), lambda i: (i, 0))
    o, gate, k_out, v_out = pl.pallas_call(
        attn_kernel,
        grid=(tokens // block,),
        in_specs=[row, whole(1, width), whole(width, heads, 2 * dim), whole(experts, width), whole(experts, width, cols), lane(1), lane(2), whole(half, 1), cache, cache],
        out_specs=[pl.BlockSpec((2, block, cols), lambda i: (0, i, 0)), lane(2), cache, cache],
        out_shape=[jax.ShapeDtypeStruct((2, tokens, cols), BF16), jax.ShapeDtypeStruct((2, tokens), F32), jax.ShapeDtypeStruct(k_t.shape, BF16), jax.ShapeDtypeStruct(v_t.shape, BF16)],
        scratch_shapes=[pltpu.VMEM((2 * heads, slots, block), F32), pltpu.VMEM((2 * heads, slots * 8, block), F32), pltpu.VMEM((width, 2 * cols), BF16)],
        compiler_params=pltpu.CompilerParams(dimension_semantics=("arbitrary",), vmem_limit_bytes=VMEM_LIMIT),
        name="attention",
    )(x, norm_att.reshape(1, width), w_kv, router_att.T, w_query, positions.reshape(1, tokens), att_ids.T, inv_freq[:, None], k_t, v_t)
    return o, gate, k_out.transpose(3, 0, 1, 2), v_out.transpose(3, 0, 1, 2)


def exchange(produce, loads, resid_hbm, out_ref, stage, pair_in, held, ring, far_in, full_in, own, resid, sel, resid_sem, swap_sem, ring_sem, d2d_sem):
    rows, width = out_ref.shape
    mine = rows // 2
    chips = lax.axis_size("tp") // 2
    piece = mine // chips
    cuts = 4
    cw = width // cuts
    me = lax.axis_index("tp")
    core = lax.rem(me, 2)
    chip = me // 2
    other = 1 - core
    right_chip = lax.rem(chip + 1, chips)
    left_chip = lax.rem(chip + chips - 1, chips)
    far_chip = lax.rem(chip + 2, chips)
    partner = {"tp": chip * 2 + other}
    right = {"tp": right_chip * 2 + core}
    left = {"tp": left_chip * 2 + core}

    barrier = pltpu.get_barrier_semaphore()
    for peer in (partner, right, left):
        pl.semaphore_signal(barrier, inc=1, device_id=peer, device_id_type=MESH)
    for copy in loads:
        copy.start()

    def first_row(c, q):
        return pl.multiple_of(c * mine + q * piece, piece)

    def rows_of(c, q):
        return pl.ds(first_row(c, q), piece)

    resid_copy = pltpu.make_async_copy(resid_hbm.at[rows_of(core, chip)], resid, resid_sem)
    resid_copy.start()
    for copy in loads:
        copy.wait()
    pending = []

    def send(src, dst, sem, peer):
        copy = pltpu.make_async_remote_copy(src_ref=src, dst_ref=dst, send_sem=sem.at[0], recv_sem=sem.at[1], device_id=peer, device_id_type=MESH)
        copy.start()
        pending.append(copy)
        return copy

    def cut(k, n=1):
        return slice(k * cw, (k + n) * cw)

    def dcut(k, n=1):
        return pl.ds(k * cw, n * cw)

    def swap(slot, i, q, k, n):
        stage[slot, :, cut(k, n)] = produce(first_row(other, q), k * cw, n * cw, sel).astype(BF16)
        if i == 0:
            pl.semaphore_wait(barrier, 3)
        copy = send(stage.at[slot, :, dcut(k, n)], pair_in.at[slot, :, dcut(k, n)], swap_sem.at[i], partner)
        held[slot, :, cut(k, n)] = produce(first_row(core, q), k * cw, n * cw, sel)
        return copy

    def land(copy, slot, k, n):
        copy.wait_recv()
        held[slot, :, cut(k, n)] += pair_in[slot, :, cut(k, n)].astype(F32)

    land(swap(0, 0, far_chip, 0, cuts), 0, 0, cuts)
    ring[0] = held[0].astype(BF16)
    far, plain, added = {}, {}, {}
    for k in (0, 2, 1, 3):
        far[k] = send(ring.at[0, :, dcut(k)], far_in.at[:, dcut(k)], ring_sem.at[k], right if k < 2 else left)
    land(swap(1, 1, right_chip, 2, 2), 1, 2, 2)
    ring[1, :, cut(2, 2)] = held[1, :, cut(2, 2)].astype(BF16)
    plain[2] = send(ring.at[1, :, dcut(2)], full_in.at[0, :, dcut(2)], ring_sem.at[6], right)
    land(swap(2, 2, left_chip, 0, 2), 2, 0, 2)
    ring[2, :, cut(0, 2)] = held[2, :, cut(0, 2)].astype(BF16)
    plain[0] = send(ring.at[2, :, dcut(0)], full_in.at[1, :, dcut(0)], ring_sem.at[4], left)
    swap_r = swap(1, 3, right_chip, 0, 2)
    swap_l = swap(2, 4, left_chip, 2, 2)
    land(swap_r, 1, 0, 2)
    land(swap_l, 2, 2, 2)

    def add_on(k):
        slot = 1 if k < 2 else 2
        far[k].wait_recv()
        ring[slot, :, cut(k)] = (held[slot, :, cut(k)] + far_in[:, cut(k)].astype(F32)).astype(BF16)
        added[k] = send(ring.at[slot, :, dcut(k)], full_in.at[slot - 1, :, dcut(k)], ring_sem.at[8 + k], right if k < 2 else left)

    add_on(0)
    add_on(2)
    add_on(1)
    add_on(3)
    plain[3] = send(ring.at[1, :, dcut(3)], full_in.at[0, :, dcut(3)], ring_sem.at[7], right)
    plain[1] = send(ring.at[2, :, dcut(1)], full_in.at[1, :, dcut(1)], ring_sem.at[5], left)
    land(swap(3, 5, chip, 0, cuts), 3, 0, cuts)
    resid_copy.wait()

    own_rows, left_rows, right_rows, far_rows = (rows_of(core, q) for q in (chip, left_chip, right_chip, far_chip))
    to_right, to_left = {}, {}
    for k in (0, 2, 1, 3):
        plain[k].wait_recv()
        added[k].wait_recv()
        own[:, cut(k)] = (resid[:, cut(k)].astype(F32) + (held[3, :, cut(k)] + full_in[0, :, cut(k)].astype(F32) + full_in[1, :, cut(k)].astype(F32))).astype(BF16)
        to_right[k] = send(own.at[:, dcut(k)], out_ref.at[own_rows, dcut(k)], ring_sem.at[12 + k], right)
        to_left[k] = send(own.at[:, dcut(k)], out_ref.at[own_rows, dcut(k)], ring_sem.at[16 + k], left)
    d2d = [send(own, out_ref.at[own_rows], d2d_sem.at[0], partner)]
    out_ref[own_rows, :] = own[...]
    onward = {}
    for k in (0, 2, 1, 3):
        to_right[k].wait_recv()
        if k < 2:
            onward[k] = send(out_ref.at[left_rows, dcut(k)], out_ref.at[left_rows, dcut(k)], ring_sem.at[20 + k], right)
        d2d.append(send(out_ref.at[left_rows, dcut(k)], out_ref.at[left_rows, dcut(k)], d2d_sem.at[1 + k], partner))
        to_left[k].wait_recv()
        if k >= 2:
            onward[k] = send(out_ref.at[right_rows, dcut(k)], out_ref.at[right_rows, dcut(k)], ring_sem.at[20 + k], left)
        d2d.append(send(out_ref.at[right_rows, dcut(k)], out_ref.at[right_rows, dcut(k)], d2d_sem.at[5 + k], partner))
    for k in (0, 2, 1, 3):
        onward[k].wait_recv()
        d2d.append(send(out_ref.at[far_rows, dcut(k)], out_ref.at[far_rows, dcut(k)], d2d_sem.at[9 + k], partner))
    for copy in d2d:
        copy.wait_recv()
    for copy in pending:
        copy.wait_send()


def load_all(pairs, sem):
    return [pltpu.make_async_copy(src, dst, sem.at[i]) for i, (src, dst) in enumerate(pairs)]


def project_kernel(o_hbm, ids_hbm, gate_hbm, wo_hbm, resid_hbm, out_ref, o_ref, ids_ref, gate_ref, wo_ref, load_sem, *rest):
    cols = o_ref.shape[2]
    experts = wo_ref.shape[0] // cols

    def produce(start, col, width, sel):
        block = sel.shape[0]
        total = None
        for j in range(2):
            ids_col = jnp.broadcast_to(ids_ref[j:j + 1, pl.ds(start, block)], (cols, block)).T
            gate_col = jnp.broadcast_to(gate_ref[j:j + 1, pl.ds(start, block)], (cols, block)).T
            o_j = o_ref[j, pl.ds(start, block), :].astype(F32)
            for e in range(experts):
                sel[:, e * cols:(e + 1) * cols] = jnp.where(ids_col == e, o_j, 0.0).astype(BF16)
            projected = jnp.dot(sel[...], wo_ref[:, col:col + width], preferred_element_type=F32)
            scaled = projected * jnp.concatenate([gate_col] * (width // cols), axis=1)
            total = scaled if total is None else total + scaled
        return total

    exchange(produce, load_all(((o_hbm, o_ref), (ids_hbm, ids_ref), (gate_hbm, gate_ref), (wo_hbm, wo_ref)), load_sem), resid_hbm, out_ref, *rest)


def combine_kernel(z_hbm, place_hbm, resid_hbm, out_ref, z_ref, place_ref, load_sem, *rest):
    def produce(start, col, width, sel):
        block = sel.shape[0]
        place = [jnp.broadcast_to(place_ref[j:j + 1, pl.ds(start, block)], (block, block)).T for j in range(2)]
        lane = lax.broadcasted_iota(jnp.int32, (block, block), 1).astype(F32)
        for r in range(0, sel.shape[1], block):
            here = lane + float(r)
            sel[:, r:r + block] = jnp.where((place[0] == here) | (place[1] == here), 1.0, 0.0).astype(BF16)
        return jnp.dot(sel[...], z_ref[:, col:col + width], preferred_element_type=F32)

    exchange(produce, load_all(((z_hbm, z_ref), (place_hbm, place_ref)), load_sem), resid_hbm, out_ref, *rest)


def reduce_call(kernel, operands, depth, resid, collective_id, name, limit):
    rows, width = resid.shape
    piece = rows // lax.axis_size("tp")
    vmem = pl.BlockSpec(memory_space=pltpu.VMEM)
    return pl.pallas_call(
        kernel,
        in_specs=[pl.BlockSpec(memory_space=pltpu.HBM)] * len(operands) + [pl.BlockSpec(memory_space=pl.ANY)],
        out_specs=vmem,
        out_shape=jax.ShapeDtypeStruct((rows, width), BF16),
        scratch_shapes=[pltpu.VMEM(op.shape, op.dtype) for op in operands] + [
            pltpu.SemaphoreType.DMA((len(operands),)),
            pltpu.VMEM((4, piece, width), BF16),
            pltpu.VMEM((4, piece, width), BF16),
            pltpu.VMEM((4, piece, width), F32),
            pltpu.VMEM((3, piece, width), BF16),
            pltpu.VMEM((piece, width), BF16),
            pltpu.VMEM((2, piece, width), BF16),
            pltpu.VMEM((piece, width), BF16),
            pltpu.VMEM((piece, width), BF16),
            pltpu.VMEM((piece, depth), BF16),
            pltpu.SemaphoreType.DMA,
            pltpu.SemaphoreType.DMA((6, 2)),
            pltpu.SemaphoreType.DMA((24, 2)),
            pltpu.SemaphoreType.DMA((13, 2)),
        ],
        compiler_params=pltpu.CompilerParams(collective_id=collective_id, has_side_effects=True, vmem_limit_bytes=limit),
        name=name,
    )(*operands, resid)


def mlp_kernel(rows, x_hbm, gain_ref, router_ref, ids_ref, wg_hbm, wu_hbm, wd_hbm, z_hbm, place_ref, x_ref, wg, wu, wd, normed, act, stage, blank, rank_ref, gate_ref, count_ref, flag_ref, sem, z_sem, blank_sem, x_sem):
    tokens, width = x_hbm.shape
    local, _, ffn = wg.shape
    experts = router_ref.shape[0]

    x_copy = pltpu.make_async_copy(x_hbm, x_ref, x_sem)
    x_copy.start()

    def weight(e, i):
        src, dst = ((wg_hbm, wg), (wu_hbm, wu), (wd_hbm, wd))[i]
        return pltpu.make_async_copy(src.at[e], dst.at[e], sem.at[e, i])

    ids_row = [ids_ref[j:j + 1, :] for j in range(2)]
    first = lax.axis_index("tp") * local
    local_iota = first + lax.broadcasted_iota(jnp.int32, (8, tokens), 0)
    hit = [(ids_row[j] == local_iota) for j in range(2)]
    member = jnp.where(hit[0] | hit[1], 1.0, 0.0)
    counts = [jnp.sum(member[e:e + 1, :]).astype(jnp.int32) for e in range(local)]
    busiest, most = jnp.int32(0), counts[0]
    for e in range(1, local):
        busiest = jnp.where(counts[e] > most, e, busiest)
        most = jnp.maximum(counts[e], most)

    def nth(i):
        return jnp.where(i == 0, busiest, jnp.where(i - 1 < busiest, i - 1, i))

    flag_ref[0] = 0
    flag_ref[1] = 0
    flag_ref[2] = 0

    def fetch():
        issued = flag_ref[2]

        @pl.when(issued < 3 * local)
        def _():
            e = nth(issued // 3)
            for i in range(3):
                @pl.when(issued % 3 == i)
                def _():
                    weight(e, i).start()
            flag_ref[2] = issued + 1

    for _ in range(3):
        fetch()

    step = 128
    blank[...] = jnp.zeros_like(blank)
    x_copy.wait()
    for t in range(0, tokens, step):
        xf = x_ref[t:t + step, :].astype(F32)
        inv = lax.rsqrt(jnp.mean(xf * xf, axis=-1, keepdims=True) + NORM_EPS)
        normed[t:t + step, :] = (xf * inv * gain_ref[...]).astype(BF16)

    logits = lax.dot_general(router_ref[...], normed[...], (((1,), (1,)), ((), ())), preferred_element_type=F32)
    expert_iota = lax.broadcasted_iota(jnp.int32, (experts, tokens), 0)
    picked = [jnp.sum(jnp.where(expert_iota == ids_row[j], logits, 0.0), axis=0, keepdims=True) for j in range(2)]
    top = jnp.maximum(picked[0], picked[1])
    raised = [jnp.exp(p - top) for p in picked]
    gate = [r / (raised[0] + raised[1]) for r in raised]
    gate_ref[...] = jnp.where(hit[0], gate[0], 0.0) + jnp.where(hit[1], gate[1], 0.0)
    tri = jnp.where(lax.broadcasted_iota(jnp.int32, (step, step), 0) <= lax.broadcasted_iota(jnp.int32, (step, step), 1), 1.0, 0.0).astype(BF16)
    running = jnp.zeros((8, 1), F32)
    for t in range(0, tokens, step):
        piece = member[:, t:t + step]
        inside = jnp.dot(piece.astype(BF16), tri, preferred_element_type=F32)
        rank_ref[:, t:t + step] = jnp.where(piece > 0, inside + running - 1.0, -1.0)
        running = running + jnp.sum(piece, axis=1, keepdims=True)

    start = jnp.int32(0)
    place = [jnp.full((1, tokens), -1.0, F32) for _ in range(2)]
    for e in range(local):
        count = counts[e]
        count_ref[e, 0] = count
        count_ref[e, 1] = start
        offset = (start * rows).astype(F32)
        place = [jnp.where(hit[j][e:e + 1, :], rank_ref[e:e + 1, :] + offset, place[j]) for j in range(2)]
        start = start + (count + rows - 1) // rows
    for j in range(2):
        place_ref[j:j + 1, :] = place[j]

    def blank_copy(i):
        return pltpu.make_async_copy(blank, z_hbm.at[pl.ds(pl.multiple_of(i * rows, rows), rows)], blank_sem)

    def z_copy(i, slot, n):
        return pltpu.make_async_copy(stage.at[slot, pl.ds(0, n * rows)], z_hbm.at[pl.ds(pl.multiple_of(i * rows, rows), n * rows)], z_sem.at[slot])

    total_tiles = z_hbm.shape[0] // rows
    used = start

    def blank_start(i, carry):
        blank_copy(i).start()
        return carry

    def tile(e, base, n, z_row):
        size = n * rows
        hits = rank_ref[pl.ds(e, 1), :] == (lax.broadcasted_iota(jnp.int32, (size, tokens), 0) + base).astype(F32)
        gate_col = jnp.sum(jnp.where(hits, gate_ref[pl.ds(e, 1), :], 0.0), axis=1, keepdims=True)
        picked_rows = jnp.dot(jnp.where(hits, 1.0, 0.0).astype(BF16), normed[...], preferred_element_type=F32).astype(BF16)
        for f in range(0, ffn, 512):
            g = jnp.dot(picked_rows, wg[e, :, f:f + 512], preferred_element_type=F32)
            u = jnp.dot(picked_rows, wu[e, :, f:f + 512], preferred_element_type=F32)
            act[:size, f:f + 512] = (jax.nn.silu(g) * u).astype(BF16)

        fetch()

        @pl.when(base == 0)
        def _():
            weight(e, 2).wait()
            fetch()

        down = jnp.dot(act[:size, :], wd[e], preferred_element_type=F32) * gate_col
        slot = n - 1

        @pl.when(flag_ref[slot] == 1)
        def _():
            z_copy(0, slot, n).wait()

        stage[slot, :size, :] = down.astype(BF16)
        z_copy(z_row, slot, n).start()
        flag_ref[slot] = 1
        fetch()

    def expert_step(turn, carry):
        e = nth(turn)
        count = count_ref[e, 0]
        begin = count_ref[e, 1]
        weight(e, 0).wait()
        fetch()
        weight(e, 1).wait()
        fetch()
        pairs = (count + rows - 1) // (2 * rows)

        def pair_step(i, inner):
            tile(e, i * (2 * rows), 2, begin + 2 * i)
            return inner

        lax.fori_loop(0, pairs, pair_step, 0)

        @pl.when(count > pairs * (2 * rows))
        def _():
            tile(e, pairs * (2 * rows), 1, begin + 2 * pairs)

        @pl.when(count == 0)
        def _():
            weight(e, 2).wait()
            fetch()

        @pl.when(turn == 0)
        def _():
            lax.fori_loop(used, total_tiles, blank_start, 0)

        return carry

    lax.fori_loop(0, local, expert_step, 0)

    def blank_wait(i, carry):
        blank_copy(i).wait()
        return carry

    lax.fori_loop(used, total_tiles, blank_wait, 0)
    for slot in range(2):
        @pl.when(flag_ref[slot] == 1)
        def _():
            z_copy(0, slot, slot + 1).wait()


def experts_mlp(x1, mlp_ids, norm_mlp, router_mlp, w_gate, w_up, w_down, rows=128):
    tokens, width = x1.shape
    local, _, ffn = w_gate.shape
    vmem = pl.BlockSpec(memory_space=pltpu.VMEM)
    hbm = pl.BlockSpec(memory_space=pl.ANY)
    return pl.pallas_call(
        functools.partial(mlp_kernel, rows),
        in_specs=[hbm, vmem, vmem, vmem, hbm, hbm, hbm],
        out_specs=[hbm, vmem],
        out_shape=[jax.ShapeDtypeStruct((2 * tokens + local * rows, width), BF16), jax.ShapeDtypeStruct((2, tokens), F32)],
        scratch_shapes=[
            pltpu.VMEM((tokens, width), BF16),
            pltpu.VMEM((local, width, ffn), BF16),
            pltpu.VMEM((local, width, ffn), BF16),
            pltpu.VMEM((local, ffn, width), BF16),
            pltpu.VMEM((tokens, width), BF16),
            pltpu.VMEM((2 * rows, ffn), BF16),
            pltpu.VMEM((2, 2 * rows, width), BF16),
            pltpu.VMEM((rows, width), BF16),
            pltpu.VMEM((8, tokens), F32),
            pltpu.VMEM((8, tokens), F32),
            pltpu.SMEM((local, 2), jnp.int32),
            pltpu.SMEM((3,), jnp.int32),
            pltpu.SemaphoreType.DMA((local, 3)),
            pltpu.SemaphoreType.DMA((2,)),
            pltpu.SemaphoreType.DMA,
            pltpu.SemaphoreType.DMA,
        ],
        compiler_params=pltpu.CompilerParams(vmem_limit_bytes=VMEM_LIMIT),
        name="experts",
    )(x1, norm_mlp.reshape(1, width), router_mlp.T, mlp_ids.T, w_gate, w_up, w_down)


def solution(mesh):
    def local_step(x, k_cache, v_cache, positions, att_ids, mlp_ids, norm_att, w_kv, router_att, w_query, w_out, norm_mlp, router_mlp, w_gate, w_up, w_down):
        o, gate, keys_all, values_all = attention(x, k_cache, v_cache, positions, att_ids, norm_att, w_kv, router_att, w_query)
        depth = w_out.shape[0] * w_out.shape[1]
        x_mid = reduce_call(project_kernel, (o, att_ids.T, gate, w_out.reshape(depth, x.shape[1])), depth, x, 0, "project", VMEM_LIMIT)
        z, place = experts_mlp(x_mid, mlp_ids, norm_mlp, router_mlp, w_gate, w_up, w_down)
        x_out = reduce_call(combine_kernel, (z, place), z.shape[0], x_mid, 1, "combine", 50 * 1024 * 1024)
        return x_out, keys_all, values_all

    token_spec = P('dp', None)
    cache_spec = P('dp', None, 'tp', None)
    expert_spec = P('tp', None, None)
    in_specs = (token_spec, cache_spec, cache_spec, P('dp'), token_spec, token_spec, P(), P(None, 'tp', None), P(), P(None, None, 'tp'), P(None, 'tp', None), P(), P(), expert_spec, expert_spec, expert_spec)
    out_specs = (token_spec, cache_spec, cache_spec)
    return jax.shard_map(local_step, mesh=mesh, in_specs=in_specs, out_specs=out_specs, check_vma=False)
```

time: 148 us -> 127 us (0.86); the launches traced: 146 us -> 128 us
  Pallas kernels: 134 us -> 125 us
  local copies, waits for them, and re-layouts: 9.32 us -> 2.01 us
  other arithmetic: 1.94 us -> 0 us
    pallas_call x1, Pallas kernels: 50 us -> 37.9 us  [attention(): pl.pallas_call(attn_kernel, grid=(tokens // block,), in_specs=[row, whole...]
    unnamed x12 -> x3, local copies, waits for them, and re-layouts: 9.32 us -> 2.01 us
    pallas_call x3, Pallas kernels: 84.2 us -> 87.2 us  [the longest x2 65.8 us: reduce_call(): pl.pallas_call(kernel, in_specs=[pl.BlockSpec(memory_space=pltpu.HBM)] *...]
where the time goes in v2:
time: 127 us; the launch traced here: 128 us
  Pallas kernels  125 us (98%)
  local copies, waits for them, and re-layouts  2.01 us (2%)
    pallas_call x2, Pallas kernels, reduce_call(): pl.pallas_call(kernel, in_specs=[pl.BlockSpec(memory_space=pltpu.HBM)] *...  65.8 us
    pallas_call x1, Pallas kernels, attention(): pl.pallas_call(attn_kernel, grid=(tokens // block,), in_specs=[row, whole...  37.9 us
    pallas_call x1, Pallas kernels, experts_mlp(): pl.pallas_call(functools.partial(mlp_kernel, rows), in_specs=[hbm, vmem,...  21.4 us

profile of v2, /device:TPU:113, one launch (start us, length us, event | category | flops | bytes accessed | tf_op | source)
XLA Modules:
  0.0 127.7 jit_solution(16058885129662710341)
XLA Ops:
  0.6 37.9 %attention.1 = (bf16[2,1024,128]{2,1,0:T(8,128)(2,1)}, f32[2,1024]{1,0:T(2,128)}, bf16[64,2,64,1024]{3,2,1,0:T(8,128)(2,1)}, bf16[64,2,64,1024]{3,2,1,0:T(8,128)(2,1)}) custom-call(bf16[1024,1024]{1,0:T(8,128)(2,1)} %resid_hbm.1, f32[1,1024]{1,0:T(1,128)} %bitcast.20, bf16[1024,2,128]{2,1,0:T(2,128)(2,1)} %wkv_ref.1, bf16[16,1024]{1,0:T(8,128)(2,1)} %bitcast.16, ...), custom_call_target="tpu_custom_call" | custom-call | tf_op jit(solution)/shard_map/attention/pallas_call | solution.py:134
  38.5 34.0 %project.1.x_hbm.resid_hbm = bf16[1024,1024]{1,0:T(8,128)(2,1)} custom-call(bf16[2,1024,128]{2,1,0:T(8,128)(2,1)} %get-tuple-element.9.o_hbm, s32[2,1024]{1,0:T(2,128)} %bitcast.18, f32[2,1024]{1,0:T(2,128)} %get-tuple-element.10.gate_hbm, bf16[2048,1024]{1,0:T(8,128)(2,1)} %bitcast.14, bf16[1024,1024]{1,0:T(8,128)(2,1)} %resid_hbm.1), custom_call_target="tpu_custom_call" | custom-call | tf_op jit(solution)/shard_map/project/pallas_call | solution.py:309
  72.5 21.4 %experts.1 = (bf16[2560,1024]{1,0:T(8,128)(2,1)}, f32[2,1024]{1,0:T(2,128)}) custom-call(bf16[1024,1024]{1,0:T(8,128)(2,1)} %project.1.x_hbm.resid_hbm, f32[1,1024]{1,0:T(1,128)} %bitcast.22, bf16[32,1024]{1,0:T(8,128)(2,1)} %bitcast.15, s32[2,1024]{1,0:T(2,128)} %bitcast.19, bf16[4,1024,2048]{2,1,0:T(8,128)(2,1)} %wg_hbm.1, bf16[4,1024,2048]{2,1,0:T(8,128)(2,1)} %wu_hbm.1, ...), custom_call_target="tpu_custom_call" | custom-call | tf_op jit(solution)/shard_map/experts/pallas_call | solution.py:506
  93.9 0.0 copy-start
  93.9 0.7 copy-done
  94.6 31.8 %combine.1 = bf16[1024,1024]{1,0:T(8,128)(2,1)S(1)} custom-call(bf16[2560,1024]{1,0:T(8,128)(2,1)} %get-tuple-element.11.z_hbm, f32[2,1024]{1,0:T(2,128)S(1)} %copy-done, bf16[1024,1024]{1,0:T(8,128)(2,1)} %project.1.x_hbm.resid_hbm), custom_call_target="tpu_custom_call" | custom-call | tf_op jit(solution)/shard_map/combine/pallas_call | solution.py:309
  126.4 1.3 %copy.21 = bf16[1024,1024]{1,0:T(8,128)(2,1)} copy(bf16[1024,1024]{1,0:T(8,128)(2,1)S(1)} %combine.1) | data formatting | bytes 4194304
Async XLA Ops:
  93.9 0.7 copy-start

commit v3 on v2

--- a/solution.py
+++ b/solution.py
@@ -144,13 +144,14 @@
     return o, gate, k_out.transpose(3, 0, 1, 2), v_out.transpose(3, 0, 1, 2)
 
 
-def exchange(produce, loads, resid_hbm, out_ref, stage, pair_in, held, ring, far_in, full_in, own, resid, sel, resid_sem, swap_sem, ring_sem, d2d_sem):
+def exchange(cuts, produce, loads, carried, resid_hbm, out_ref, stage, pair_in, held, ring, far_in, full_in, own, resid, sel, resid_sem, swap_sem, ring_sem, d2d_sem):
     rows, width = out_ref.shape
     mine = rows // 2
     chips = lax.axis_size("tp") // 2
     piece = mine // chips
-    cuts = 4
-    cw = width // cuts
+    cw = piece // cuts
+    near = cuts // 2
+    order = [k for pair in zip(range(near), range(near, cuts)) for k in pair]
     me = lax.axis_index("tp")
     core = lax.rem(me, 2)
     chip = me // 2
@@ -178,6 +179,8 @@
     resid_copy.start()
     for copy in loads:
         copy.wait()
+    for copy in carried:
+        copy.start()
     pending = []
 
     def send(src, dst, sem, peer):
@@ -186,78 +189,80 @@
         pending.append(copy)
         return copy
 
-    def cut(k, n=1):
-        return slice(k * cw, (k + n) * cw)
-
-    def dcut(k, n=1):
-        return pl.ds(k * cw, n * cw)
-
-    def swap(slot, i, q, k, n):
-        stage[slot, :, cut(k, n)] = produce(first_row(other, q), k * cw, n * cw, sel).astype(BF16)
-        if i == 0:
+    def cut(k):
+        return slice(k * cw, (k + 1) * cw)
+
+    def dcut(k):
+        return pl.ds(k * cw, cw)
+
+    def swap(slot, q):
+        stage[slot] = produce(first_row(other, q), 0, width, sel).astype(BF16)
+        if slot == 0:
             pl.semaphore_wait(barrier, 3)
-        copy = send(stage.at[slot, :, dcut(k, n)], pair_in.at[slot, :, dcut(k, n)], swap_sem.at[i], partner)
-        held[slot, :, cut(k, n)] = produce(first_row(core, q), k * cw, n * cw, sel)
+        copy = send(stage.at[slot], pair_in.at[slot], swap_sem.at[slot], partner)
+        held[slot] = produce(first_row(core, q), 0, width, sel)
         return copy
 
-    def land(copy, slot, k, n):
+    def land(copy, slot):
         copy.wait_recv()
-        held[slot, :, cut(k, n)] += pair_in[slot, :, cut(k, n)].astype(F32)
-
-    land(swap(0, 0, far_chip, 0, cuts), 0, 0, cuts)
+        held[slot] += pair_in[slot].astype(F32)
+
+    far, plain, added = {}, {}, {}
+    land(swap(0, far_chip), 0)
     ring[0] = held[0].astype(BF16)
-    far, plain, added = {}, {}, {}
-    for k in (0, 2, 1, 3):
-        far[k] = send(ring.at[0, :, dcut(k)], far_in.at[:, dcut(k)], ring_sem.at[k], right if k < 2 else left)
-    land(swap(1, 1, right_chip, 2, 2), 1, 2, 2)
-    ring[1, :, cut(2, 2)] = held[1, :, cut(2, 2)].astype(BF16)
-    plain[2] = send(ring.at[1, :, dcut(2)], full_in.at[0, :, dcut(2)], ring_sem.at[6], right)
-    land(swap(2, 2, left_chip, 0, 2), 2, 0, 2)
-    ring[2, :, cut(0, 2)] = held[2, :, cut(0, 2)].astype(BF16)
-    plain[0] = send(ring.at[2, :, dcut(0)], full_in.at[1, :, dcut(0)], ring_sem.at[4], left)
-    swap_r = swap(1, 3, right_chip, 0, 2)
-    swap_l = swap(2, 4, left_chip, 2, 2)
-    land(swap_r, 1, 0, 2)
-    land(swap_l, 2, 2, 2)
-
-    def add_on(k):
-        slot = 1 if k < 2 else 2
+    for k in order:
+        far[k] = send(ring.at[0, dcut(k)], far_in.at[dcut(k)], ring_sem.at[k], right if k < near else left)
+    land(swap(1, right_chip), 1)
+    ring[1, near * cw:] = held[1, near * cw:].astype(BF16)
+    for k in range(near, cuts):
+        plain[k] = send(ring.at[1, dcut(k)], full_in.at[0, dcut(k)], ring_sem.at[cuts + k], right)
+    land(swap(2, left_chip), 2)
+    ring[2, :near * cw] = held[2, :near * cw].astype(BF16)
+    for k in range(near):
+        plain[k] = send(ring.at[2, dcut(k)], full_in.at[1, dcut(k)], ring_sem.at[cuts + k], left)
+    for k in order:
+        slot = 1 if k < near else 2
         far[k].wait_recv()
-        ring[slot, :, cut(k)] = (held[slot, :, cut(k)] + far_in[:, cut(k)].astype(F32)).astype(BF16)
-        added[k] = send(ring.at[slot, :, dcut(k)], full_in.at[slot - 1, :, dcut(k)], ring_sem.at[8 + k], right if k < 2 else left)
-
-    add_on(0)
-    add_on(2)
-    add_on(1)
-    add_on(3)
-    plain[3] = send(ring.at[1, :, dcut(3)], full_in.at[0, :, dcut(3)], ring_sem.at[7], right)
-    plain[1] = send(ring.at[2, :, dcut(1)], full_in.at[1, :, dcut(1)], ring_sem.at[5], left)
-    land(swap(3, 5, chip, 0, cuts), 3, 0, cuts)
+        ring[slot, cut(k)] = (held[slot, cut(k)] + far_in[cut(k)].astype(F32)).astype(BF16)
+        added[k] = send(ring.at[slot, dcut(k)], full_in.at[slot - 1, dcut(k)], ring_sem.at[2 * cuts + k], right if k < near else left)
+    land(swap(3, chip), 3)
     resid_copy.wait()
 
     own_rows, left_rows, right_rows, far_rows = (rows_of(core, q) for q in (chip, left_chip, right_chip, far_chip))
     to_right, to_left = {}, {}
-    for k in (0, 2, 1, 3):
+
+    def inside(rows_start, k):
+        return pl.ds(pl.multiple_of(rows_start + k * cw, cw), cw)
+
+    own_row, left_row, right_row, far_row = (first_row(core, q) for q in (chip, left_chip, right_chip, far_chip))
+    for k in order:
         plain[k].wait_recv()
         added[k].wait_recv()
-        own[:, cut(k)] = (resid[:, cut(k)].astype(F32) + (held[3, :, cut(k)] + full_in[0, :, cut(k)].astype(F32) + full_in[1, :, cut(k)].astype(F32))).astype(BF16)
-        to_right[k] = send(own.at[:, dcut(k)], out_ref.at[own_rows, dcut(k)], ring_sem.at[12 + k], right)
-        to_left[k] = send(own.at[:, dcut(k)], out_ref.at[own_rows, dcut(k)], ring_sem.at[16 + k], left)
+        own[cut(k), :] = (resid[cut(k), :].astype(F32) + (held[3, cut(k), :] + full_in[0, cut(k), :].astype(F32) + full_in[1, cut(k), :].astype(F32))).astype(BF16)
+        first, second = ((right, to_right, 3), (left, to_left, 4))[::1 if k < near else -1]
+        for peer, table, base in (first, second):
+            table[k] = send(own.at[dcut(k)], out_ref.at[inside(own_row, k)], ring_sem.at[base * cuts + k], peer)
     d2d = [send(own, out_ref.at[own_rows], d2d_sem.at[0], partner)]
     out_ref[own_rows, :] = own[...]
     onward = {}
-    for k in (0, 2, 1, 3):
+    for k in order:
+        if k < near:
+            to_right[k].wait_recv()
+            onward[k] = send(out_ref.at[inside(left_row, k)], out_ref.at[inside(left_row, k)], ring_sem.at[5 * cuts + k], right)
+        else:
+            to_left[k].wait_recv()
+            onward[k] = send(out_ref.at[inside(right_row, k)], out_ref.at[inside(right_row, k)], ring_sem.at[5 * cuts + k], left)
+    for k in range(near, cuts):
         to_right[k].wait_recv()
-        if k < 2:
-            onward[k] = send(out_ref.at[left_rows, dcut(k)], out_ref.at[left_rows, dcut(k)], ring_sem.at[20 + k], right)
-        d2d.append(send(out_ref.at[left_rows, dcut(k)], out_ref.at[left_rows, dcut(k)], d2d_sem.at[1 + k], partner))
+    d2d.append(send(out_ref.at[left_rows], out_ref.at[left_rows], d2d_sem.at[1], partner))
+    for k in range(near):
         to_left[k].wait_recv()
-        if k >= 2:
-            onward[k] = send(out_ref.at[right_rows, dcut(k)], out_ref.at[right_rows, dcut(k)], ring_sem.at[20 + k], left)
-        d2d.append(send(out_ref.at[right_rows, dcut(k)], out_ref.at[right_rows, dcut(k)], d2d_sem.at[5 + k], partner))
-    for k in (0, 2, 1, 3):
+    d2d.append(send(out_ref.at[right_rows], out_ref.at[right_rows], d2d_sem.at[2], partner))
+    for i, k in enumerate(order):
         onward[k].wait_recv()
-        d2d.append(send(out_ref.at[far_rows, dcut(k)], out_ref.at[far_rows, dcut(k)], d2d_sem.at[9 + k], partner))
+        d2d.append(send(out_ref.at[inside(far_row, k)], out_ref.at[inside(far_row, k)], d2d_sem.at[3 + i], partner))
+    for copy in carried:
+        copy.wait()
     for copy in d2d:
         copy.wait_recv()
     for copy in pending:
@@ -268,7 +273,7 @@
     return [pltpu.make_async_copy(src, dst, sem.at[i]) for i, (src, dst) in enumerate(pairs)]
 
 
-def project_kernel(o_hbm, ids_hbm, gate_hbm, wo_hbm, resid_hbm, out_ref, o_ref, ids_ref, gate_ref, wo_ref, load_sem, *rest):
+def project_kernel(o_hbm, ids_hbm, gate_hbm, wo_hbm, wg_hbm, wu_hbm, resid_hbm, out_ref, wg_ref, wu_ref, o_ref, ids_ref, gate_ref, wo_ref, load_sem, carry_sem, *rest):
     cols = o_ref.shape[2]
     experts = wo_ref.shape[0] // cols
 
@@ -286,10 +291,10 @@
             total = scaled if total is None else total + scaled
         return total
 
-    exchange(produce, load_all(((o_hbm, o_ref), (ids_hbm, ids_ref), (gate_hbm, gate_ref), (wo_hbm, wo_ref)), load_sem), resid_hbm, out_ref, *rest)
-
-
-def combine_kernel(z_hbm, place_hbm, resid_hbm, out_ref, z_ref, place_ref, load_sem, *rest):
+    exchange(4, produce, load_all(((o_hbm, o_ref), (ids_hbm, ids_ref), (gate_hbm, gate_ref), (wo_hbm, wo_ref)), load_sem), load_all(((wg_hbm, wg_ref), (wu_hbm, wu_ref)), carry_sem), resid_hbm, out_ref, *rest)
+
+
+def combine_kernel(z_hbm, place_hbm, resid_hbm, out_ref, z_ref, place_ref, load_sem, carry_sem, *rest):
     def produce(start, col, width, sel):
         block = sel.shape[0]
         place = [jnp.broadcast_to(place_ref[j:j + 1, pl.ds(start, block)], (block, block)).T for j in range(2)]
@@ -299,20 +304,21 @@
             sel[:, r:r + block] = jnp.where((place[0] == here) | (place[1] == here), 1.0, 0.0).astype(BF16)
         return jnp.dot(sel[...], z_ref[:, col:col + width], preferred_element_type=F32)
 
-    exchange(produce, load_all(((z_hbm, z_ref), (place_hbm, place_ref)), load_sem), resid_hbm, out_ref, *rest)
-
-
-def reduce_call(kernel, operands, depth, resid, collective_id, name, limit):
+    exchange(4, produce, load_all(((z_hbm, z_ref), (place_hbm, place_ref)), load_sem), [], resid_hbm, out_ref, *rest)
+
+
+def reduce_call(kernel, operands, depth, resid, collective_id, name, limit, carried=()):
     rows, width = resid.shape
     piece = rows // lax.axis_size("tp")
     vmem = pl.BlockSpec(memory_space=pltpu.VMEM)
     return pl.pallas_call(
         kernel,
-        in_specs=[pl.BlockSpec(memory_space=pltpu.HBM)] * len(operands) + [pl.BlockSpec(memory_space=pl.ANY)],
-        out_specs=vmem,
-        out_shape=jax.ShapeDtypeStruct((rows, width), BF16),
+        in_specs=[pl.BlockSpec(memory_space=pltpu.HBM)] * (len(operands) + len(carried)) + [pl.BlockSpec(memory_space=pl.ANY)],
+        out_specs=[vmem] * (1 + len(carried)),
+        out_shape=[jax.ShapeDtypeStruct(resid.shape, BF16)] + [pltpu.VMEM(a.shape, a.dtype) for a in carried],
         scratch_shapes=[pltpu.VMEM(op.shape, op.dtype) for op in operands] + [
             pltpu.SemaphoreType.DMA((len(operands),)),
+            pltpu.SemaphoreType.DMA((2,)),
             pltpu.VMEM((4, piece, width), BF16),
             pltpu.VMEM((4, piece, width), BF16),
             pltpu.VMEM((4, piece, width), F32),
@@ -323,16 +329,16 @@
             pltpu.VMEM((piece, width), BF16),
             pltpu.VMEM((piece, depth), BF16),
             pltpu.SemaphoreType.DMA,
-            pltpu.SemaphoreType.DMA((6, 2)),
+            pltpu.SemaphoreType.DMA((4, 2)),
             pltpu.SemaphoreType.DMA((24, 2)),
             pltpu.SemaphoreType.DMA((13, 2)),
         ],
         compiler_params=pltpu.CompilerParams(collective_id=collective_id, has_side_effects=True, vmem_limit_bytes=limit),
         name=name,
-    )(*operands, resid)
-
-
-def mlp_kernel(rows, x_hbm, gain_ref, router_ref, ids_ref, wg_hbm, wu_hbm, wd_hbm, z_hbm, place_ref, x_ref, wg, wu, wd, normed, act, stage, blank, rank_ref, gate_ref, count_ref, flag_ref, sem, z_sem, blank_sem, x_sem):
+    )(*operands, *carried, resid)
+
+
+def mlp_kernel(rows, x_hbm, gain_ref, router_ref, ids_ref, wg, wu, wd_hbm, z_hbm, place_ref, x_ref, wd, normed, act, stage, blank, rank_ref, gate_ref, count_ref, flag_ref, sem, z_sem, blank_sem, x_sem):
     tokens, width = x_hbm.shape
     local, _, ffn = wg.shape
     experts = router_ref.shape[0]
@@ -340,9 +346,8 @@
     x_copy = pltpu.make_async_copy(x_hbm, x_ref, x_sem)
     x_copy.start()
 
-    def weight(e, i):
-        src, dst = ((wg_hbm, wg), (wu_hbm, wu), (wd_hbm, wd))[i]
-        return pltpu.make_async_copy(src.at[e], dst.at[e], sem.at[e, i])
+    def weight(e):
+        return pltpu.make_async_copy(wd_hbm.at[e], wd.at[e], sem.at[e])
 
     ids_row = [ids_ref[j:j + 1, :] for j in range(2)]
     first = lax.axis_index("tp") * local
@@ -365,16 +370,12 @@
     def fetch():
         issued = flag_ref[2]
 
-        @pl.when(issued < 3 * local)
-        def _():
-            e = nth(issued // 3)
-            for i in range(3):
-                @pl.when(issued % 3 == i)
-                def _():
-                    weight(e, i).start()
+        @pl.when(issued < local)
+        def _():
+            weight(nth(issued)).start()
             flag_ref[2] = issued + 1
 
-    for _ in range(3):
+    for _ in range(2):
         fetch()
 
     step = 128
@@ -439,7 +440,7 @@
 
         @pl.when(base == 0)
         def _():
-            weight(e, 2).wait()
+            weight(e).wait()
             fetch()
 
         down = jnp.dot(act[:size, :], wd[e], preferred_element_type=F32) * gate_col
@@ -458,10 +459,6 @@
         e = nth(turn)
         count = count_ref[e, 0]
         begin = count_ref[e, 1]
-        weight(e, 0).wait()
-        fetch()
-        weight(e, 1).wait()
-        fetch()
         pairs = (count + rows - 1) // (2 * rows)
 
         def pair_step(i, inner):
@@ -476,7 +473,7 @@
 
         @pl.when(count == 0)
         def _():
-            weight(e, 2).wait()
+            weight(e).wait()
             fetch()
 
         @pl.when(turn == 0)
@@ -505,13 +502,11 @@
     hbm = pl.BlockSpec(memory_space=pl.ANY)
     return pl.pallas_call(
         functools.partial(mlp_kernel, rows),
-        in_specs=[hbm, vmem, vmem, vmem, hbm, hbm, hbm],
+        in_specs=[hbm, vmem, vmem, vmem, vmem, vmem, hbm],
         out_specs=[hbm, vmem],
         out_shape=[jax.ShapeDtypeStruct((2 * tokens + local * rows, width), BF16), jax.ShapeDtypeStruct((2, tokens), F32)],
         scratch_shapes=[
             pltpu.VMEM((tokens, width), BF16),
-            pltpu.VMEM((local, width, ffn), BF16),
-            pltpu.VMEM((local, width, ffn), BF16),
             pltpu.VMEM((local, ffn, width), BF16),
             pltpu.VMEM((tokens, width), BF16),
             pltpu.VMEM((2 * rows, ffn), BF16),
@@ -521,23 +516,23 @@
             pltpu.VMEM((8, tokens), F32),
             pltpu.SMEM((local, 2), jnp.int32),
             pltpu.SMEM((3,), jnp.int32),
-            pltpu.SemaphoreType.DMA((local, 3)),
+            pltpu.SemaphoreType.DMA((local,)),
             pltpu.SemaphoreType.DMA((2,)),
             pltpu.SemaphoreType.DMA,
             pltpu.SemaphoreType.DMA,
         ],
-        compiler_params=pltpu.CompilerParams(vmem_limit_bytes=VMEM_LIMIT),
+        compiler_params=pltpu.CompilerParams(vmem_limit_bytes=27 * 1024 * 1024),
         name="experts",
-    )(x1, norm_mlp.reshape(1, width), router_mlp.T, mlp_ids.T, w_gate, w_up, w_down)
+    )(x1, norm_mlp.reshape(1, width), router_mlp.T, mlp_ids.T, pltpu.with_memory_space_constraint(w_gate, pltpu.VMEM), pltpu.with_memory_space_constraint(w_up, pltpu.VMEM), w_down)
 
 
 def solution(mesh):
     def local_step(x, k_cache, v_cache, positions, att_ids, mlp_ids, norm_att, w_kv, router_att, w_query, w_out, norm_mlp, router_mlp, w_gate, w_up, w_down):
         o, gate, keys_all, values_all = attention(x, k_cache, v_cache, positions, att_ids, norm_att, w_kv, router_att, w_query)
         depth = w_out.shape[0] * w_out.shape[1]
-        x_mid = reduce_call(project_kernel, (o, att_ids.T, gate, w_out.reshape(depth, x.shape[1])), depth, x, 0, "project", VMEM_LIMIT)
+        x_mid, w_gate, w_up = reduce_call(project_kernel, (o, att_ids.T, gate, w_out.reshape(depth, x.shape[1])), depth, x, 0, "project", 27 * 1024 * 1024, (w_gate, w_up))
         z, place = experts_mlp(x_mid, mlp_ids, norm_mlp, router_mlp, w_gate, w_up, w_down)
-        x_out = reduce_call(combine_kernel, (z, place), z.shape[0], x_mid, 1, "combine", 50 * 1024 * 1024)
+        x_out, = reduce_call(combine_kernel, (z, place), z.shape[0], x_mid, 1, "combine", 50 * 1024 * 1024)
         return x_out, keys_all, values_all
 
     token_spec = P('dp', None)

time: 127 us -> 124 us (0.976); the launches traced: 128 us -> 123 us
  Pallas kernels: 125 us -> 120 us
    pallas_call x1, Pallas kernels: 21.4 us -> 14.9 us  [experts_mlp(): pl.pallas_call(functools.partial(mlp_kernel, rows), in_specs=[hbm, vmem,...]
    pallas_call x2, Pallas kernels: 65.8 us -> 67.7 us  [reduce_call(): pl.pallas_call(kernel, in_specs=[pl.BlockSpec(memory_space=pltpu.HBM)] *...]
where the time goes in v3:
time: 124 us; the launch traced here: 123 us
  Pallas kernels  120 us (97%)
  local copies, waits for them, and re-layouts  2.01 us (2%)
    pallas_call x2, Pallas kernels, reduce_call(): pl.pallas_call(kernel, in_specs=[pl.BlockSpec(memory_space=pltpu.HBM)] *...  67.7 us
    pallas_call x1, Pallas kernels, attention(): pl.pallas_call(attn_kernel, grid=(tokens // block,), in_specs=[row, whole...  37.8 us
    pallas_call x1, Pallas kernels, experts_mlp(): pl.pallas_call(functools.partial(mlp_kernel, rows), in_specs=[hbm, vmem,...  14.9 us

profile of v3, /device:TPU:113, one launch (start us, length us, event | category | flops | bytes accessed | tf_op | source)
XLA Modules:
  0.0 123.1 jit_solution(13376649121737360492)
XLA Ops:
  0.6 37.8 %attention.1 = (bf16[2,1024,128]{2,1,0:T(8,128)(2,1)}, f32[2,1024]{1,0:T(2,128)}, bf16[64,2,64,1024]{3,2,1,0:T(8,128)(2,1)}, bf16[64,2,64,1024]{3,2,1,0:T(8,128)(2,1)}) custom-call(bf16[1024,1024]{1,0:T(8,128)(2,1)} %resid_hbm.1, f32[1,1024]{1,0:T(1,128)} %bitcast.20, bf16[1024,2,128]{2,1,0:T(2,128)(2,1)} %wkv_ref.1, bf16[16,1024]{1,0:T(8,128)(2,1)} %bitcast.16, ...), custom_call_target="tpu_custom_call" | custom-call | tf_op jit(solution)/shard_map/attention/pallas_call | solution.py:134
  38.5 33.7 %project.1 = (bf16[1024,1024]{1,0:T(8,128)(2,1)}, bf16[4,1024,2048]{2,1,0:T(8,128)(2,1)S(1)}, bf16[4,1024,2048]{2,1,0:T(8,128)(2,1)S(1)}) custom-call(bf16[2,1024,128]{2,1,0:T(8,128)(2,1)} %get-tuple-element.12.o_hbm, s32[2,1024]{1,0:T(2,128)} %bitcast.18, f32[2,1024]{1,0:T(2,128)} %get-tuple-element.13.gate_hbm, bf16[2048,1024]{1,0:T(8,128)(2,1)} %bitcast.14, ...), custom_call_target="tpu_custom_call" | custom-call | tf_op jit(solution)/shard_map/project/pallas_call | solution.py:314
  72.1 14.9 %experts.1 = (bf16[2560,1024]{1,0:T(8,128)(2,1)}, f32[2,1024]{1,0:T(2,128)}) custom-call(bf16[1024,1024]{1,0:T(8,128)(2,1)} %get-tuple-element.14.x_hbm.resid_hbm, f32[1,1024]{1,0:T(1,128)} %bitcast.22, bf16[32,1024]{1,0:T(8,128)(2,1)} %bitcast.15, s32[2,1024]{1,0:T(2,128)} %bitcast.19, bf16[4,1024,2048]{2,1,0:T(8,128)(2,1)S(1)} %get-tuple-element.15.wg, ...), custom_call_target="tpu_custom_call" | custom-call | tf_op jit(solution)/shard_map/experts/pallas_call | solution.py:503
  87.0 0.0 copy-start
  87.0 0.7 copy-done
  87.7 34.1 %combine.1 = bf16[1024,1024]{1,0:T(8,128)(2,1)S(1)} custom-call(bf16[2560,1024]{1,0:T(8,128)(2,1)} %get-tuple-element.17.z_hbm, f32[2,1024]{1,0:T(2,128)S(1)} %copy-done, bf16[1024,1024]{1,0:T(8,128)(2,1)} %get-tuple-element.14.x_hbm.resid_hbm), custom_call_target="tpu_custom_call" | custom-call | tf_op jit(solution)/shard_map/combine/pallas_call | solution.py:314
  121.8 1.3 %copy.21 = bf16[1024,1024]{1,0:T(8,128)(2,1)} copy(bf16[1024,1024]{1,0:T(8,128)(2,1)S(1)} %combine.1) | data formatting | bytes 4194304
Async XLA Ops:
  87.0 0.7 copy-start

commit v4 on v3

--- a/solution.py
+++ b/solution.py
@@ -80,7 +80,7 @@
             ko_ref[s, n] = jnp.where(at_slot, k_new[n], packed)
         return carry
 
-    lax.fori_loop(0, slots, score_step, 0, unroll=4)
+    lax.fori_loop(0, slots, score_step, 0, unroll=16)
 
     slot_iota = lax.broadcasted_iota(jnp.int32, (slots, block), 0)
     here = slot_iota == pos
@@ -112,7 +112,7 @@
             vo_ref[s, n] = jnp.where(at_slot, v_new[n], packed)
         return tuple(carry)
 
-    out = lax.fori_loop(0, slots, value_step, tuple(out), unroll=4)
+    out = lax.fori_loop(0, slots, value_step, tuple(out), unroll=16)
 
     for j in range(2):
         o_ref[j] = jnp.concatenate(out[j * heads:(j + 1) * heads], axis=0).T.astype(BF16)
@@ -307,13 +307,13 @@
     exchange(4, produce, load_all(((z_hbm, z_ref), (place_hbm, place_ref)), load_sem), [], resid_hbm, out_ref, *rest)
 
 
-def reduce_call(kernel, operands, depth, resid, collective_id, name, limit, carried=()):
+def reduce_call(kernel, operands, depth, resid, collective_id, name, limit, spaces, carried=()):
     rows, width = resid.shape
     piece = rows // lax.axis_size("tp")
     vmem = pl.BlockSpec(memory_space=pltpu.VMEM)
     return pl.pallas_call(
         kernel,
-        in_specs=[pl.BlockSpec(memory_space=pltpu.HBM)] * (len(operands) + len(carried)) + [pl.BlockSpec(memory_space=pl.ANY)],
+        in_specs=[pl.BlockSpec(memory_space=space) for space in spaces] + [pl.BlockSpec(memory_space=pltpu.HBM)] * len(carried) + [pl.BlockSpec(memory_space=pl.ANY)],
         out_specs=[vmem] * (1 + len(carried)),
         out_shape=[jax.ShapeDtypeStruct(resid.shape, BF16)] + [pltpu.VMEM(a.shape, a.dtype) for a in carried],
         scratch_shapes=[pltpu.VMEM(op.shape, op.dtype) for op in operands] + [
@@ -504,7 +504,7 @@
         functools.partial(mlp_kernel, rows),
         in_specs=[hbm, vmem, vmem, vmem, vmem, vmem, hbm],
         out_specs=[hbm, vmem],
-        out_shape=[jax.ShapeDtypeStruct((2 * tokens + local * rows, width), BF16), jax.ShapeDtypeStruct((2, tokens), F32)],
+        out_shape=[jax.ShapeDtypeStruct((2 * tokens + local * rows, width), BF16), pltpu.VMEM((2, tokens), F32)],
         scratch_shapes=[
             pltpu.VMEM((tokens, width), BF16),
             pltpu.VMEM((local, ffn, width), BF16),
@@ -530,9 +530,9 @@
     def local_step(x, k_cache, v_cache, positions, att_ids, mlp_ids, norm_att, w_kv, router_att, w_query, w_out, norm_mlp, router_mlp, w_gate, w_up, w_down):
         o, gate, keys_all, values_all = attention(x, k_cache, v_cache, positions, att_ids, norm_att, w_kv, router_att, w_query)
         depth = w_out.shape[0] * w_out.shape[1]
-        x_mid, w_gate, w_up = reduce_call(project_kernel, (o, att_ids.T, gate, w_out.reshape(depth, x.shape[1])), depth, x, 0, "project", 27 * 1024 * 1024, (w_gate, w_up))
+        x_mid, w_gate, w_up = reduce_call(project_kernel, (o, att_ids.T, gate, w_out.reshape(depth, x.shape[1])), depth, x, 0, "project", 27 * 1024 * 1024, (pltpu.HBM,) * 4, (w_gate, w_up))
         z, place = experts_mlp(x_mid, mlp_ids, norm_mlp, router_mlp, w_gate, w_up, w_down)
-        x_out, = reduce_call(combine_kernel, (z, place), z.shape[0], x_mid, 1, "combine", 50 * 1024 * 1024)
+        x_out, = reduce_call(combine_kernel, (z, pltpu.with_memory_space_constraint(place, pltpu.VMEM)), z.shape[0], x_mid, 1, "combine", 50 * 1024 * 1024, (pltpu.HBM, pltpu.VMEM))
         return x_out, keys_all, values_all
 
     token_spec = P('dp', None)

time: 124 us -> 123 us (level); the launches traced: 123 us -> 120 us
  Pallas kernels: 120 us -> 118 us
    pallas_call x2, Pallas kernels: 67.7 us -> 60.8 us  [reduce_call(): pl.pallas_call(kernel, in_specs=[pl.BlockSpec(memory_space=space) for spa...]
    pallas_call x1, Pallas kernels: 14.9 us -> 20.3 us  [experts_mlp(): pl.pallas_call(functools.partial(mlp_kernel, rows), in_specs=[hbm, vmem,...]
where the time goes in v4:
time: 123 us; the launch traced here: 120 us
  Pallas kernels  118 us (96%)
  local copies, waits for them, and re-layouts  1.32 us (1%)
    pallas_call x2, Pallas kernels, reduce_call(): pl.pallas_call(kernel, in_specs=[pl.BlockSpec(memory_space=space) for spa...  60.8 us
    pallas_call x1, Pallas kernels, attention(): pl.pallas_call(attn_kernel, grid=(tokens // block,), in_specs=[row, whole...  37.1 us
    pallas_call x1, Pallas kernels, experts_mlp(): pl.pallas_call(functools.partial(mlp_kernel, rows), in_specs=[hbm, vmem,...  20.3 us

profile of v4, /device:TPU:113, one launch (start us, length us, event | category | flops | bytes accessed | tf_op | source)
XLA Modules:
  0.0 120.2 jit_solution(5719552376430001593)
XLA Ops:
  0.6 37.1 %attention.1 = (bf16[2,1024,128]{2,1,0:T(8,128)(2,1)}, f32[2,1024]{1,0:T(2,128)}, bf16[64,2,64,1024]{3,2,1,0:T(8,128)(2,1)}, bf16[64,2,64,1024]{3,2,1,0:T(8,128)(2,1)}) custom-call(bf16[1024,1024]{1,0:T(8,128)(2,1)} %resid_hbm.1, f32[1,1024]{1,0:T(1,128)} %bitcast.20, bf16[1024,2,128]{2,1,0:T(2,128)(2,1)} %wkv_ref.1, bf16[16,1024]{1,0:T(8,128)(2,1)} %bitcast.16, ...), custom_call_target="tpu_custom_call" | custom-call | tf_op jit(solution)/shard_map/attention/pallas_call | solution.py:134
  37.7 33.7 %project.1 = (bf16[1024,1024]{1,0:T(8,128)(2,1)}, bf16[4,1024,2048]{2,1,0:T(8,128)(2,1)S(1)}, bf16[4,1024,2048]{2,1,0:T(8,128)(2,1)S(1)}) custom-call(bf16[2,1024,128]{2,1,0:T(8,128)(2,1)} %get-tuple-element.12.o_hbm, s32[2,1024]{1,0:T(2,128)} %bitcast.18, f32[2,1024]{1,0:T(2,128)} %get-tuple-element.13.gate_hbm, bf16[2048,1024]{1,0:T(8,128)(2,1)} %bitcast.14, ...), custom_call_target="tpu_custom_call" | custom-call | tf_op jit(solution)/shard_map/project/pallas_call | solution.py:314
  71.4 20.3 %experts.1 = (bf16[2560,1024]{1,0:T(8,128)(2,1)}, f32[2,1024]{1,0:T(2,128)S(1)}) custom-call(bf16[1024,1024]{1,0:T(8,128)(2,1)} %get-tuple-element.14.x_hbm.resid_hbm, f32[1,1024]{1,0:T(1,128)} %bitcast.22, bf16[32,1024]{1,0:T(8,128)(2,1)} %bitcast.15, s32[2,1024]{1,0:T(2,128)} %bitcast.19, bf16[4,1024,2048]{2,1,0:T(8,128)(2,1)S(1)} %get-tuple-element.15.wg, ...), custom_call_target="tpu_custom_call" | custom-call | tf_op jit(solution)/shard_map/experts/pallas_call | solution.py:503
  91.7 27.1 %combine.1 = bf16[1024,1024]{1,0:T(8,128)(2,1)S(1)} custom-call(bf16[2560,1024]{1,0:T(8,128)(2,1)} %get-tuple-element.17.z_hbm, f32[2,1024]{1,0:T(2,128)S(1)} %get-tuple-element.18.place_hbm, bf16[1024,1024]{1,0:T(8,128)(2,1)} %get-tuple-element.14.x_hbm.resid_hbm), custom_call_target="tpu_custom_call" | custom-call | tf_op jit(solution)/shard_map/combine/pallas_call | solution.py:314
  118.8 1.3 %copy.21 = bf16[1024,1024]{1,0:T(8,128)(2,1)} copy(bf16[1024,1024]{1,0:T(8,128)(2,1)S(1)} %combine.1) | data formatting | bytes 4194304
